TPU v7x, 128 devices: a whole 4x4x4 slice. The times are simulated.
128 devices in a mesh: row: 16 (over x_hi, y, core), col: 4 (over z), dp: 2 (over x_lo).
Axes of the slice: x: 4 (x_hi: 2, x_lo: 2; x = x_hi * 2 + x_lo), y: 4, z: 4, core: 2. Of those that a mesh axis runs over, the one named last changes fastest.
Arguments:
- slides: bfloat16 [2, 256, 128, 512], P('dp', 'row', 'col'), may hold values from -6 to 6
- cotangent: bfloat16 [2, 256, 128, 512], P('dp', 'row', 'col'), may hold values from -6 to 6
- kernel: float32 [2, 7, 7, 512], replicated, may hold values from -0.875 to 0.875
- kernel_bias: float32 [2, 512], replicated, may hold values from -3 to 3
- norm_gain: float32 [2, 512], replicated, may hold values from 0.1 to 1.9
- norm_bias: float32 [2, 512], replicated, may hold values from -3 to 3
- weight_in: bfloat16 [2, 512, 2048], P(None, 'dp'), may hold values from -0.25 to 0.25
- bias_in: float32 [2, 2048], replicated, may hold values from -3 to 3
- weight_out: bfloat16 [2, 2048, 512], P(None, None, 'dp'), may hold values from -0.125 to 0.125
- bias_out: float32 [2, 512], replicated, may hold values from -3 to 3
- layer_scale: float32 [2, 512], replicated, may hold values from 0.3 to 1.5
Outputs:
- output: bfloat16 [2, 256, 128, 512], P('dp', 'row', 'col')
- grad_slides: bfloat16 [2, 256, 128, 512], P('dp', 'row', 'col')
- grad_weight_in: float32 [2, 512, 2048], P(None, 'dp')
- grad_weight_out: float32 [2, 2048, 512], P(None, None, 'dp')
- grad_kernel: float32 [2, 7, 7, 512], replicated
- grad_channel: float32 [2, 5, 512], replicated
- grad_bias_in: float32 [2, 2048], replicated
All inputs are finite; a program needn't handle non-finite values.
Results may differ from a plain program's by a relative error of at most 0.01.
Values may be sent and summed in bfloat16 or wider, within the bound.
No kernel may reach another device: no remote copies, remote signals or barrier semaphores. Data moves between devices by JAX's collectives and lax.ppermute only.
A program may use at most 128 MiB of HBM per device.

v0:
```python
import jax
import jax.numpy as jnp
from jax import lax
from jax.experimental import pallas as pl
from jax.experimental.pallas import tpu as pltpu
from jax.sharding import PartitionSpec as P

COEF = 0.7978845608028654
CUBIC = 0.044715
EPSILON = 1e-06

PIX = 512
CH = 512
FF = 2048
HALF = 1024
WIRE = FF + 128
ROWS, COLS = 16, 32
WIDE = 40
DEEP = 14
SLAB = DEEP * WIDE * 8
SPACE = ("xh", "y", "z")
F32, BF16 = jnp.float32, jnp.bfloat16

VM = pl.BlockSpec(memory_space=pltpu.VMEM)
SM = pl.BlockSpec(memory_space=pltpu.SMEM)


def call(body, outs, count, flops, scratch=(), scalars=0):
    shapes = [jax.ShapeDtypeStruct(s, d) for s, d in outs]
    return pl.pallas_call(
        body,
        out_shape=shapes,
        in_specs=[SM] * scalars + [VM] * (count - scalars),
        out_specs=[VM] * len(outs),
        scratch_shapes=list(scratch),
        compiler_params=pltpu.CompilerParams(vmem_limit_bytes=56 * 1024 * 1024),
        cost_estimate=pl.CostEstimate(
            flops=flops, bytes_accessed=4_000_000, transcendentals=0
        ),
    )


def at(row, col):
    return (row * WIDE + col) * 8


def homes(row):
    found = []
    if row < DEEP:
        found.append((0, row))
    if row >= 8:
        found.append((1, row - 8))
    return found


def put_row(slab, row, line):
    for block, inner in homes(row):
        for group in range(4):
            slab[pl.ds(at(inner, 3) + block * 4 + group, COLS, stride=8), :] = line[
                :, group * 128 : (group + 1) * 128
            ]


def put_edges(slab, top, bottom):
    for k in range(3):
        put_row(slab, k, top[k * COLS : (k + 1) * COLS, :].astype(F32))
        put_row(slab, 19 + k, bottom[k * COLS : (k + 1) * COLS, :].astype(F32))


def put_columns(slab, left, right):
    for row in range(DEEP):
        a, b = row * 24, (row + 1) * 24
        slab[pl.ds(at(row, 0), 24), :] = left[a:b, :].astype(F32)
        slab[pl.ds(at(row, 35), 24), :] = right[a:b, :].astype(F32)


def take_columns(slab, to_low, to_high):
    for row in range(DEEP):
        a, b = row * 24, (row + 1) * 24
        to_low[a:b, :] = slab[pl.ds(at(row, 3), 24), :].astype(BF16)
        to_high[a:b, :] = slab[pl.ds(at(row, 32), 24), :].astype(BF16)


def filtered(slab, taps, store):
    def step(n, carry):
        row = n // 4
        col = (n % 4) * 8
        sums = [None] * 8
        for p in range(7):
            base = pl.multiple_of(((row + p) * WIDE + col) * 8, 8)
            seen = [slab[pl.ds(base + 8 * k, 8), :] for k in range(14)]
            for q in range(7):
                weight = taps[(p * 7 + q) * 8 : (p * 7 + q + 1) * 8, :]
                for m in range(8):
                    term = seen[m + q] * weight
                    sums[m] = term if sums[m] is None else sums[m] + term
        base = pl.multiple_of((row * COLS + col) * 8, 8)
        for m in range(8):
            store[pl.ds(base + 8 * m, 8), :] = sums[m]
        return carry

    lax.fori_loop(0, 32, step, 0)


def line_of(store, row):
    block, inner = row // 8, row % 8
    return jnp.concatenate(
        [
            store[pl.ds(inner * COLS * 8 + block * 4 + group, COLS, stride=8), :]
            for group in range(4)
        ],
        axis=1,
    )


def pack_body(x, top, bottom, slab, to_low, to_high):
    for row in range(ROWS):
        put_row(slab, row + 3, x[row * COLS : (row + 1) * COLS, :].astype(F32))
    put_edges(slab, top, bottom)
    take_columns(slab, to_low, to_high)


def edge_body(old, top, bottom, slab, to_low, to_high):
    slab[...] = old[...]
    put_edges(slab, top, bottom)
    take_columns(slab, to_low, to_high)


def norm_body(old, left, right, taps, bias, gain, shift, slab, normal, normed, rstd, store):
    slab[...] = old[...]
    put_columns(slab, left, right)
    filtered(slab, taps, store)
    for row in range(ROWS):
        a, b = row * COLS, (row + 1) * COLS
        mixed = line_of(store, row) + bias[...]
        center = mixed - jnp.mean(mixed, -1, keepdims=True)
        scale = lax.rsqrt(jnp.mean(center * center, -1, keepdims=True) + EPSILON)
        value = center * scale
        normed[a:b, :] = value
        rstd[a:b, :] = jnp.broadcast_to(scale, (COLS, 128))
        normal[a:b, :] = (value * gain[...] + shift[...]).astype(BF16)


def mlp_body(
    place, a, normal, own_in, got_in, mate_in, own_out, got_out, mate_out,
    bias_in, bias_out, scale,
    out, top, bottom, act, slope, branch, full_in, full_out,
):
    core, part = place[0], place[1]
    mine = pl.multiple_of(part * 256, 256)
    theirs = pl.multiple_of((1 - part) * 256, 256)
    full_in[pl.ds(mine, 256), :] = own_in[...]
    full_in[pl.ds(pl.multiple_of(theirs + core * 128, 128), 128), :] = got_in[...]
    full_in[pl.ds(pl.multiple_of(theirs + (1 - core) * 128, 128), 128), :] = mate_in[...]
    full_out[:, pl.ds(mine, 256)] = own_out[...]
    full_out[pl.ds(pl.multiple_of(core * HALF, HALF), HALF), pl.ds(theirs, 256)] = got_out[...]
    full_out[pl.ds(pl.multiple_of((1 - core) * HALF, HALF), HALF), pl.ds(theirs, 256)] = mate_out[...]
    for c in range(8):
        cols = slice(c * 256, (c + 1) * 256)
        hidden = jnp.dot(normal[...], full_in[:, cols], preferred_element_type=F32)
        v = hidden + bias_in[:, cols]
        square = v * v
        tangent = jnp.tanh(v * (COEF + (COEF * CUBIC) * square))
        half = 0.5 * v
        act[:, cols] = (half + half * tangent).astype(BF16)
        slope[:, cols] = (
            0.5
            + 0.5 * tangent
            + half * (1.0 - tangent * tangent) * (COEF + (3.0 * COEF * CUBIC) * square)
        ).astype(BF16)
    for c in range(2):
        cols = slice(c * 256, (c + 1) * 256)
        value = jnp.dot(act[...], full_out[:, cols], preferred_element_type=F32)
        value = value + bias_out[:, cols]
        branch[:, cols] = value
        result = (a[:, cols].astype(F32) + scale[:, cols] * value).astype(BF16)
        out[:, cols] = result
        top[:, cols] = result[:96, :]
        bottom[:, cols] = result[416:, :]


def back_body(
    place, u, branch, act, slope, normal, normed, rstd, full_in, full_out, gain, scale,
    keep, give, slab, top, bottom, channel, bias, low, gh, gn,
):
    core = place[0]
    rows_first = (((0,), (0,)), ((), ()))
    cols_last = (((1,), (1,)), ((), ()))
    up = u[...].astype(F32)
    channel[4:5, :] = jnp.sum(up * branch[...], 0, keepdims=True)
    gb = up * scale[...]
    channel[3:4, :] = jnp.sum(gb, 0, keepdims=True)
    low[...] = gb.astype(BF16)
    for c in range(8):
        cols = slice(c * 256, (c + 1) * 256)
        ga = lax.dot_general(
            low[...], full_out[cols, :], cols_last, preferred_element_type=F32
        )
        value = ga * slope[:, cols].astype(F32)
        bias[:, cols] = jnp.sum(value, 0, keepdims=True)
        gh[:, cols] = value.astype(BF16)
    for side, ref in ((core, keep), (1 - core, give)):
        for c in range(4):
            cols = pl.ds(pl.multiple_of(side * HALF + c * 256, 256), 256)
            ref[:, c * 256 : (c + 1) * 256] = lax.dot_general(
                normal[...], gh[:, cols], rows_first, preferred_element_type=F32
            ).astype(BF16)
            ref[:, HALF + c * 256 : HALF + (c + 1) * 256] = lax.dot_general(
                low[...], act[:, cols], rows_first, preferred_element_type=F32
            ).astype(BF16)
    for c in range(2):
        cols = slice(c * 256, (c + 1) * 256)
        gn[:, cols] = lax.dot_general(
            gh[...], full_in[cols, :], cols_last, preferred_element_type=F32
        )
    sums = [jnp.zeros((8, CH), F32) for _ in range(3)]

    def folded(value):
        return value[0:8] + value[8:16] + value[16:24] + value[24:32]

    for row in range(ROWS):
        a, b = row * COLS, (row + 1) * COLS
        grad = gn[a:b, :]
        value = normed[a:b, :]
        sums[1] += folded(grad * value)
        sums[2] += folded(grad)
        gs = grad * gain[...]
        gm = rstd[a:b, 0:1] * (
            gs
            - jnp.mean(gs, -1, keepdims=True)
            - value * jnp.mean(gs * value, -1, keepdims=True)
        )
        sums[0] += folded(gm)
        put_row(slab, row + 3, gm)
        if row < 3:
            top[a:b, :] = gm.astype(BF16)
        if row >= 13:
            bottom[a - 416 : b - 416, :] = gm.astype(BF16)
    for k in range(3):
        channel[k : k + 1, :] = jnp.sum(sums[k], 0, keepdims=True)


def taps_body(seen, grads, out):
    for p in range(7):

        def step(n, sums, p=p):
            row = n // 4
            col = (n % 4) * 8
            base = pl.multiple_of(((row + p) * WIDE + col) * 8, 8)
            home = pl.multiple_of(((row + 3) * WIDE + col + 3) * 8, 8)
            near = [seen[pl.ds(base + 8 * k, 8), :] for k in range(14)]
            sums = list(sums)
            for m in range(8):
                grad = grads[pl.ds(home + 8 * m, 8), :]
                for q in range(7):
                    sums[q] = sums[q] + near[m + q] * grad
            return tuple(sums)

        sums = lax.fori_loop(0, 32, step, tuple(jnp.zeros((8, 128), F32) for _ in range(7)))
        for q in range(7):
            out[(p * 7 + q) * 4 : (p * 7 + q + 1) * 4, :] = sums[q][0:4] + sums[q][4:8]


def up_body(old, left, right, taps, u, out, slab, store):
    slab[...] = old[...]
    put_columns(slab, left, right)
    filtered(slab, taps, store)
    for row in range(ROWS):
        a, b = row * COLS, (row + 1) * COLS
        out[a:b, :] = (u[a:b, :].astype(F32) + line_of(store, row)).astype(out.dtype)


def pair_body(keep, got, taps, channel, bias, out, lines):
    lines[0:196, :] = taps[...]
    spot = 196
    for kind in range(5):
        for group in range(4):
            lines[spot : spot + 1, :] = channel[
                kind : kind + 1, group * 128 : (group + 1) * 128
            ]
            spot += 1
    for group in range(16):
        lines[spot : spot + 1, :] = bias[:, group * 128 : (group + 1) * 128]
        spot += 1
    lines[spot:256, :] = jnp.zeros((256 - spot, 128), F32)

    def step(n, carry):
        rows = pl.ds(pl.multiple_of(n * 32, 32), 32)
        total = keep[rows, :].astype(F32) + got[rows, :].astype(F32)
        out[pl.ds(n * 4, 4), :, :FF] = total.reshape(4, 8, FF).astype(BF16)
        rows = pl.ds(pl.multiple_of((n % 8) * 32, 32), 32)
        out[pl.ds(n * 4, 4), :, FF:] = lines[rows, :].reshape(4, 8, 128).astype(BF16)
        return carry

    lax.fori_loop(0, 16, step, 0)


def merge_body(pieces0, pieces1, out):
    for k, pieces in ((0, pieces0), (1, pieces1)):
        for a, b in ((0, 512), (512, 1024), (1024, 1536), (1536, 2176)):
            def step(n, total, a=a, b=b, pieces=pieces):
                for m in range(4):
                    total = total + pieces[n * 4 + m, :, a:b].astype(F32)
                return total

            total = lax.fori_loop(0, 16, step, jnp.zeros((8, b - a), F32)).astype(BF16)
            for n in range(32):
                out[n, :, k * WIRE + a : k * WIRE + b] = total


def small_body(whole0, whole1, mate0, mate1, taps, channel, bias, lines):
    for k, whole, mate in ((0, whole0, mate0), (1, whole1, mate1)):
        lines[0:256, :] = (whole[...].astype(F32) + mate[...].astype(F32)).reshape(256, 128)
        for group in range(4):
            cols = slice(group * 128, (group + 1) * 128)
            taps[k, :, cols] = lines[pl.ds(group, 49, stride=4), :]
            channel[k, :, cols] = lines[pl.ds(196 + group, 5, stride=4), :]
        for group in range(16):
            bias[k : k + 1, group * 128 : (group + 1) * 128] = lines[216 + group : 217 + group, :]


def finish_body(place, whole, mate, grad_in, grad_out):
    core = place[0]
    for side, ref in ((core, whole), (1 - core, mate)):
        span = pl.ds(pl.multiple_of(side * HALF, HALF), HALF)
        value = ref[:, :, :FF].astype(F32).reshape(128, FF)
        grad_in[0, :, span] = value[:, :HALF]
        grad_out[0, span, :] = value[:, HALF:].T


STORE = pltpu.VMEM((ROWS * COLS * 4 + 16, 128), F32)
STRIP = ((DEEP * 24, 128), BF16)
EDGE = ((96, CH), BF16)


def pack(x, top, bottom):
    return call(pack_body, [((SLAB, 128), F32), STRIP, STRIP], 3, 10_000_000)(x, top, bottom)


def pack_edges(slab, top, bottom):
    return call(edge_body, [((SLAB, 128), F32), STRIP, STRIP], 3, 10_000_000)(slab, top, bottom)


def normalise(slab, left, right, taps, bias, gain, shift):
    outs = [((SLAB, 128), F32), ((PIX, CH), BF16), ((PIX, CH), F32), ((PIX, 128), F32)]
    return call(norm_body, outs, 7, 40_000_000, [STORE])(
        slab, left, right, taps, bias, gain, shift
    )


def mlp(place, a, normal, weights, bias_in, bias_out, scale):
    outs = [
        ((PIX, CH), BF16), EDGE, EDGE, ((PIX, FF), BF16), ((PIX, FF), BF16),
        ((PIX, CH), F32), ((CH, FF), BF16), ((FF, CH), BF16),
    ]
    return call(mlp_body, outs, 12, 60_000_000, scalars=1)(
        place, a, normal, *weights, bias_in, bias_out, scale
    )


def backward(place, u, saved, gain, scale):
    outs = [
        ((CH, FF), BF16), ((CH, FF), BF16), ((SLAB, 128), F32), EDGE, EDGE,
        ((8, CH), F32), ((1, FF), F32),
    ]
    scratch = [
        pltpu.VMEM((PIX, CH), BF16), pltpu.VMEM((PIX, FF), BF16), pltpu.VMEM((PIX, CH), F32),
    ]
    return call(back_body, outs, 12, 100_000_000, scratch, scalars=1)(
        place, u, *saved, gain, scale
    )


def tap_grads(seen, grads):
    return call(taps_body, [((49 * 4, 128), F32)], 2, 40_000_000)(seen, grads)[0]


def upstream(slab, left, right, taps, u, dtype):
    scratch = [pltpu.VMEM((SLAB, 128), F32), STORE]
    return call(up_body, [((PIX, CH), dtype)], 5, 40_000_000, scratch)(
        slab, left, right, taps, u
    )[0]


def spread(taps):
    lines = taps.reshape(49, 1, 4, 128)
    return jnp.broadcast_to(lines, (49, 2, 4, 128)).reshape(49 * 8, 128)


def finish(place, whole, mate):
    block = pl.BlockSpec((16, 8, WIRE), lambda layer, i: (i, 0, layer))
    return pl.pallas_call(
        finish_body,
        grid=(2, 2),
        out_shape=[
            jax.ShapeDtypeStruct((2, 256, FF), F32),
            jax.ShapeDtypeStruct((2, FF, 256), F32),
        ],
        in_specs=[SM, block, block],
        out_specs=[
            pl.BlockSpec((1, 128, FF), lambda layer, i: (layer, i, 0)),
            pl.BlockSpec((1, FF, 128), lambda layer, i: (layer, 0, i)),
        ],
        cost_estimate=pl.CostEstimate(
            flops=10_000_000, bytes_accessed=12_000_000, transcendentals=0
        ),
    )(place, whole, mate)


def finish_small(whole, mate):
    first = pl.BlockSpec((32, 8, 128), lambda i: (0, 0, FF // 128))
    second = pl.BlockSpec((32, 8, 128), lambda i: (0, 0, (WIRE + FF) // 128))
    shapes = [(2, 49, CH), (2, 5, CH), (2, FF)]
    return pl.pallas_call(
        small_body,
        grid=(1,),
        out_shape=[jax.ShapeDtypeStruct(s, F32) for s in shapes],
        in_specs=[first, second, first, second],
        out_specs=[
            pl.BlockSpec((2, 49, CH), lambda i: (0, 0, 0)),
            pl.BlockSpec((2, 5, CH), lambda i: (0, 0, 0)),
            pl.BlockSpec((2, FF), lambda i: (0, 0)),
        ],
        scratch_shapes=[pltpu.VMEM((256 + 8, 128), F32)],
        cost_estimate=pl.CostEstimate(
            flops=1_000_000, bytes_accessed=1_000_000, transcendentals=0
        ),
    )(whole, whole, mate, mate)


RANKS = ("xh", "y", "core")
FORWARD = {"rows": [(i, i + 1) for i in range(15)], "z": [(i, i + 1) for i in range(3)]}
BACKWARD = {k: [(b, a) for a, b in v] for k, v in FORWARD.items()}


def from_rows(top, bottom):
    above = lax.ppermute(bottom, RANKS, FORWARD["rows"])
    below = lax.ppermute(top, RANKS, BACKWARD["rows"])
    return above, below


def from_columns(to_low, to_high):
    left = lax.ppermute(to_high, "z", FORWARD["z"])
    right = lax.ppermute(to_low, "z", BACKWARD["z"])
    return left, right


def swapped(value, axis):
    return lax.ppermute(value, axis, [(0, 1), (1, 0)])


def around_x(value, step):
    return lax.ppermute(value, ("xh", "dp"), [(i, (i + step) % 4) for i in range(4)])


def fetch_weights(core, weight_in, weight_out, k):
    half_in = lax.dynamic_slice(weight_in, (k, core * 128, 0), (1, 128, FF))[0]
    half_out = lax.dynamic_slice(weight_out, (k, core * HALF, 0), (1, HALF, 256))[0]
    got_in = around_x(half_in, 1)
    got_out = around_x(half_out, -1)
    mate_in = swapped(got_in, "core")
    mate_out = swapped(got_out, "core")
    return weight_in[k], got_in, mate_in, weight_out[k], got_out, mate_out


def send_grads(keep, got, taps, channel, bias):
    scratch = [pltpu.VMEM((256, 128), F32)]
    pair = call(pair_body, [((64, 8, WIRE), BF16)], 5, 2_000_000, scratch)(
        keep, got, taps, channel, bias
    )[0]
    return lax.all_to_all(pair, ("dp", *SPACE), 0, 0, tiled=True)


def per_device(
    slides,
    cotangent,
    kernel,
    kernel_bias,
    norm_gain,
    norm_bias,
    weight_in,
    bias_in,
    weight_out,
    bias_out,
    layer_scale,
):
    core, part = lax.axis_index("core"), lax.axis_index("dp")
    place = jnp.stack([core, part]).astype(jnp.int32)
    one = lambda table, which: table[which][None]
    current = slides.reshape(PIX, CH)
    top, bottom = current[:96], current[416:]
    saved = []
    slabs = []
    weights = fetch_weights(core, weight_in, weight_out, 0)
    for k in range(2):
        above, below = from_rows(top, bottom)
        slab, to_low, to_high = pack(current, above, below)
        left, right = from_columns(to_low, to_high)
        slab, normal, normed, rstd = normalise(
            slab, left, right, spread(kernel[k]),
            one(kernel_bias, k), one(norm_gain, k), one(norm_bias, k),
        )
        current, top, bottom, act, slope, branch, full_in, full_out = mlp(
            place, current, normal, weights,
            one(bias_in, k), one(bias_out, k), one(layer_scale, k),
        )
        slabs.append(slab)
        saved.append((branch, act, slope, normal, normed, rstd, full_in, full_out))
        if k == 0:
            later_in, later_out, _ = lax.optimization_barrier((weight_in, weight_out, left))
            weights = fetch_weights(core, later_in, later_out, 1)
    up = cotangent.reshape(PIX, CH)
    pieces = [None] * 2
    for k in (1, 0):
        keep, give, grads, top, bottom, channel, bias = backward(
            place, up, saved[k], one(norm_gain, k), one(layer_scale, k)
        )
        got = swapped(give, "core")
        above, below = from_rows(top, bottom)
        taps = tap_grads(slabs[k], grads)
        pieces[k] = send_grads(keep, got, taps, channel, bias)
        slab, to_low, to_high = pack_edges(grads, above, below)
        left, right = from_columns(to_low, to_high)
        up = upstream(
            slab, left, right, spread(kernel[k][::-1, ::-1]), up, F32 if k else BF16
        )
    copies = call(merge_body, [((32, 8, 2 * WIRE), BF16)], 2, 5_000_000)(*pieces)[0]
    whole = lax.all_to_all(copies, SPACE, 0, 0, tiled=True)
    mate = swapped(whole, "core")
    grad_in, grad_out = finish(place, whole, mate)
    grad_taps, grad_channel, grad_bias = finish_small(whole, mate)
    return (
        current.reshape(slides.shape),
        up.reshape(slides.shape),
        grad_in,
        grad_out,
        grad_taps.reshape(2, 7, 7, CH),
        grad_channel,
        grad_bias,
    )


def solution(mesh):
    fine = jax.sharding.Mesh(
        mesh.devices.reshape(2, 4, 2, 4, 2), ("xh", "y", "core", "z", "dp")
    )
    maps = P("dp", RANKS, "z", None)
    split_in, split_out = P(None, "dp", None), P(None, None, "dp")
    whole = P()
    return jax.shard_map(
        per_device,
        mesh=fine,
        in_specs=(
            maps, maps, whole, whole, whole, whole, split_in, whole, split_out, whole, whole,
        ),
        out_specs=(maps, maps, split_in, split_out, whole, whole, whole),
        check_vma=False,
    )
```

profile of v0, /device:TPU:1, one launch (start us, length us, event | category | flops | bytes accessed | tf_op | source)
XLA Modules:
  0.0 322.4 jit_solution(11461624475814863977)
XLA Ops:
  0.6 1.7 fusion
  2.4 4.6 %collective-permute-start = (bf16[96,512]{1,0:T(8,128)(2,1)}, bf16[96,512]{1,0:T(8,128)(2,1)}, u32[]{:S(2)}, u32[]{:S(2)}) collective-permute-start(bf16[96,512]{1,0:T(8,128)(2,1)} %bitcast.3), channel_id=1, source_target_pairs={{0,8},{8,16},{16,24},{24,32},{32,40},{40,48},{48,56},{56,64},{64,7... | collective-permute-start | bytes 294920 | tf_op jit(solution)/shard_map/ppermute | solution.py:437
  7.0 1.9 collective-permute-start.1
  8.9 1.9 dynamic-slice_bitcast_fusion.3
  12.0 2.0 dynamic-slice_bitcast_fusion.2
  14.0 1.5 collective-permute-start.6
  19.1 2.8 shard_map.162
  21.9 3.5 %collective-permute-start.2 = (bf16[336,128]{1,0:T(8,128)(2,1)}, bf16[336,128]{1,0:T(8,128)(2,1)S(1)}, u32[]{:S(2)}, u32[]{:S(2)}) collective-permute-start(bf16[336,128]{1,0:T(8,128)(2,1)} %get-tuple-element.63), channel_id=1, source_target_pairs={{0,2},{2,4},{4,6},{1,3},{3,5},{5,7},{8,10},{10,12},{12,14},{9,11},... | collective-permute-start | bytes 258056 | tf_op jit(solution)/shard_map/ppermute | solution.py:443
  28.4 2.7 collective-permute-start.14
  31.2 5.7 %collective-permute-start.5 = (bf16[128,2048]{1,0:T(8,128)(2,1)S(1)}, bf16[128,2048]{1,0:T(8,128)(2,1)S(1)}, u32[]{:S(2)}, u32[]{:S(2)}) collective-permute-start(bf16[128,2048]{1,0:T(8,128)(2,1)S(1)} %collective-permute-done.4.got_in), channel_id=1, source_target_pairs={{0,8},{8,0},{1,9},{9,1},{2,10},{10,2},{3,11},{11,3},{4,12},{12,4},... | collective-permute-start | bytes 1572872 | tf_op jit(solution)/shard_map/ppermute | solution.py:449
  39.5 4.5 %collective-permute-done.3.right = bf16[336,128]{1,0:T(8,128)(2,1)S(1)} collective-permute-done((bf16[336,128]{1,0:T(8,128)(2,1)S(1)}, bf16[336,128]{1,0:T(8,128)(2,1)S(1)}, u32[]{:S(2)}, u32[]{:S(2)}) %collective-permute-start.3) | collective-permute-done | bytes 86048 | tf_op jit(solution)/shard_map/ppermute | solution.py:444
  44.8 9.1 %shard_map.163 = (f32[4480,128]{1,0:T(8,128)}, bf16[512,512]{1,0:T(8,128)(2,1)}, f32[512,512]{1,0:T(8,128)}, f32[512,128]{1,0:T(8,128)}) custom-call(f32[4480,128]{1,0:T(8,128)} %get-tuple-element.62.old, bf16[336,128]{1,0:T(8,128)(2,1)} %copy-done.26, bf16[336,128]{1,0:T(8,128)(2,1)} %copy-done.29, f32[392,128]{1,0:T(8,128)} %bitcast.44, ...), custom_call_target="tpu_custom_call" | custom-call | flops 40000000 | bytes 4000000 | tf_op jit(solution)/shard_map/pallas_call | solution.py:346
  56.1 10.5 %shard_map.164 = (bf16[512,512]{1,0:T(8,128)(2,1)}, bf16[96,512]{1,0:T(8,128)(2,1)}, bf16[96,512]{1,0:T(8,128)(2,1)}, bf16[512,2048]{1,0:T(8,128)(2,1)}, bf16[51...) custom-call(s32[2]{0:T(128)} %pad_add_fusion.place, ...), custom_call_target="tpu_custom_call" | custom-call | flops 60000000 | bytes 4000000 | tf_op jit(solution)/shard_map/pallas_call | solution.py:356
  66.6 2.1 collective-permute-start.8
  68.6 2.4 collective-permute-start.9
  72.1 2.7 collective-permute-done.9.bottom
  75.4 2.8 shard_map.165
  78.2 3.5 %collective-permute-start.10 = (bf16[336,128]{1,0:T(8,128)(2,1)}, bf16[336,128]{1,0:T(8,128)(2,1)S(1)}, u32[]{:S(2)}, u32[]{:S(2)}) collective-permute-start(bf16[336,128]{1,0:T(8,128)(2,1)} %get-tuple-element.70), channel_id=1, source_target_pairs={{0,2},{2,4},{4,6},{1,3},{3,5},{5,7},{8,10},{10,12},{12,14},{9,11},... | collective-permute-start | bytes 258056 | tf_op jit(solution)/shard_map/ppermute | solution.py:443
  84.3 2.9 collective-permute-done.11.right
  87.9 9.0 %shard_map.166 = (f32[4480,128]{1,0:T(8,128)}, bf16[512,512]{1,0:T(8,128)(2,1)}, f32[512,512]{1,0:T(8,128)}, f32[512,128]{1,0:T(8,128)}) custom-call(f32[4480,128]{1,0:T(8,128)} %get-tuple-element.69.old, bf16[336,128]{1,0:T(8,128)(2,1)} %copy-done.27, bf16[336,128]{1,0:T(8,128)(2,1)} %copy-done.28, f32[392,128]{1,0:T(8,128)} %bitcast.43, ...), custom_call_target="tpu_custom_call" | custom-call | flops 40000000 | bytes 4000000 | tf_op jit(solution)/shard_map/pallas_call | solution.py:346
  97.9 10.5 %shard_map.167 = (bf16[512,512]{1,0:T(8,128)(2,1)}, bf16[96,512]{1,0:T(8,128)(2,1)}, bf16[96,512]{1,0:T(8,128)(2,1)}, bf16[512,2048]{1,0:T(8,128)(2,1)}, bf16[51...) custom-call(s32[2]{0:T(128)} %pad_add_fusion.place, ...), custom_call_target="tpu_custom_call" | custom-call | flops 60000000 | bytes 4000000 | tf_op jit(solution)/shard_map/pallas_call | solution.py:356
  108.4 11.4 %shard_map.168 = (bf16[512,2048]{1,0:T(8,128)(2,1)}, bf16[512,2048]{1,0:T(8,128)(2,1)}, f32[4480,128]{1,0:T(8,128)}, bf16[96,512]{1,0:T(8,128)(2,1)}, bf16[96,51...) custom-call(s32[2]{0:T(128)} %pad_add_fusion.place, bf16[512,512]{1,0:T(8,128)(2,1)} %bitcast.37, ...), custom_call_target="tpu_custom_call" | custom-call | flops 100000000 | bytes 4000000 | tf_op jit(solution)/shard_map/pallas_call | solution.py:369
  119.8 3.4 %collective-permute-start.16 = (bf16[96,512]{1,0:T(8,128)(2,1)}, bf16[96,512]{1,0:T(8,128)(2,1)S(1)}, u32[]{:S(2)}, u32[]{:S(2)}) collective-permute-start(bf16[96,512]{1,0:T(8,128)(2,1)} %get-tuple-element.84), channel_id=1, source_target_pairs={{0,8},{8,16},{16,24},{24,32},{32,40},{40,48},{48,56},{56,64},{64,7... | collective-permute-start | bytes 294920 | tf_op jit(solution)/shard_map/ppermute | solution.py:437
  123.2 1.9 collective-permute-start.17
  125.1 9.0 %shard_map.176.taps = f32[196,128]{1,0:T(8,128)} custom-call(f32[4480,128]{1,0:T(8,128)} %get-tuple-element.109.seen, f32[4480,128]{1,0:T(8,128)} %get-tuple-element.83.old.grads), custom_call_target="tpu_custom_call" | custom-call | flops 40000000 | bytes 4000000 | tf_op jit(solution)/shard_map/pallas_call | solution.py:375
  135.4 3.3 %shard_map.169 = (f32[4480,128]{1,0:T(8,128)}, bf16[336,128]{1,0:T(8,128)(2,1)}, bf16[336,128]{1,0:T(8,128)(2,1)}) custom-call(f32[4480,128]{1,0:T(8,128)} %get-tuple-element.83.old.grads, bf16[96,512]{1,0:T(8,128)(2,1)} %copy-done.16, bf16[96,512]{1,0:T(8,128)(2,1)} %copy-done.18), custom_call_target="tpu_custom_call" | custom-call | flops 10000000 | bytes 4000000 | tf_op jit(solution)/shard_map/pallas_call | solution.py:341
  138.7 3.3 %collective-permute-start.18 = (bf16[336,128]{1,0:T(8,128)(2,1)}, bf16[336,128]{1,0:T(8,128)(2,1)S(1)}, u32[]{:S(2)}, u32[]{:S(2)}) collective-permute-start(bf16[336,128]{1,0:T(8,128)(2,1)} %get-tuple-element.87), channel_id=1, source_target_pairs={{0,2},{2,4},{4,6},{1,3},{3,5},{5,7},{8,10},{10,12},{12,14},{9,11},... | collective-permute-start | bytes 258056 | tf_op jit(solution)/shard_map/ppermute | solution.py:443
  144.7 4.2 %shard_map.177 = bf16[64,8,2176]{2,1,0:T(8,128)(2,1)} custom-call(bf16[512,2048]{1,0:T(8,128)(2,1)} %get-tuple-element.107.keep, bf16[512,2048]{1,0:T(8,128)(2,1)} %copy-done.5, f32[196,128]{1,0:T(8,128)} %shard_map.176.taps, f32[8,512]{1,0:T(8,128)} %get-tuple-element.110.channel, f32[1,2048]{1,0:T(1,128)} %get-tuple-element.111.bias), custom_call_target="tpu_custom_call" | custom-call | flops 2000000 | bytes 4000000 | tf_op jit(solution)/shard_map/pallas_call | solution.py:468
  148.9 11.6 %all-to-all-start.1 = ((bf16[64,8,2176]{2,1,0:T(8,128)(2,1)}), bf16[64,8,2176]{2,1,0:T(8,128)(2,1)S(1)}, u32[]{:S(2)}, u32[]{:S(2)}) async-start(bf16[64,8,2176]{2,1,0:T(8,128)(2,1)} %shard_map.177), calls=%async_computation.1 | async-start | bytes 4456448 | tf_op jit(solution)/shard_map/all_to_all | solution.py:471
  161.5 7.8 %shard_map.170.u = f32[512,512]{1,0:T(8,128)} custom-call(f32[4480,128]{1,0:T(8,128)} %get-tuple-element.86.old, bf16[336,128]{1,0:T(8,128)(2,1)} %copy-done.22, bf16[336,128]{1,0:T(8,128)(2,1)} %copy-done.23, f32[392,128]{1,0:T(8,128)} %bitcast.42, bf16[512,512]{1,0:T(8,128)(2,1)} %bitcast.38), custom_call_target="tpu_custom_call" | custom-call | flops 40000000 | bytes 4000000 | tf_op jit(solution)/shard_map/pallas_call | solution.py:380
  169.3 11.6 %shard_map.171 = (bf16[512,2048]{1,0:T(8,128)(2,1)}, bf16[512,2048]{1,0:T(8,128)(2,1)}, f32[4480,128]{1,0:T(8,128)}, bf16[96,512]{1,0:T(8,128)(2,1)}, bf16[96,51...) custom-call(s32[2]{0:T(128)} %pad_add_fusion.place, f32[512,512]{1,0:T(8,128)} %shard_map.170.u, ...), custom_call_target="tpu_custom_call" | custom-call | flops 100000000 | bytes 4000000 | tf_op jit(solution)/shard_map/pallas_call | solution.py:369
  180.8 3.5 %collective-permute-start.24 = (bf16[512,2048]{1,0:T(8,128)(2,1)}, bf16[512,2048]{1,0:T(8,128)(2,1)S(1)}, u32[]{:S(2)}, u32[]{:S(2)}) collective-permute-start(bf16[512,2048]{1,0:T(8,128)(2,1)} %get-tuple-element.103), channel_id=1, source_target_pairs={{0,8},{8,0},{1,9},{9,1},{2,10},{10,2},{3,11},{11,3},{4,12},{12,4},... | collective-permute-start | bytes 6291464 | tf_op jit(solution)/shard_map/ppermute | solution.py:449
  184.4 9.0 %shard_map.174.taps = f32[196,128]{1,0:T(8,128)} custom-call(f32[4480,128]{1,0:T(8,128)} %get-tuple-element.104.seen, f32[4480,128]{1,0:T(8,128)} %get-tuple-element.96.old.grads), custom_call_target="tpu_custom_call" | custom-call | flops 40000000 | bytes 4000000 | tf_op jit(solution)/shard_map/pallas_call | solution.py:375
  194.7 4.2 %shard_map.175 = bf16[64,8,2176]{2,1,0:T(8,128)(2,1)} custom-call(bf16[512,2048]{1,0:T(8,128)(2,1)} %get-tuple-element.102.keep, bf16[512,2048]{1,0:T(8,128)(2,1)} %copy-done.6, f32[196,128]{1,0:T(8,128)} %shard_map.174.taps, f32[8,512]{1,0:T(8,128)} %get-tuple-element.105.channel, f32[1,2048]{1,0:T(1,128)} %get-tuple-element.106.bias), custom_call_target="tpu_custom_call" | custom-call | flops 2000000 | bytes 4000000 | tf_op jit(solution)/shard_map/pallas_call | solution.py:468
  198.9 42.3 %all_to_all.15.pieces0 = bf16[64,8,2176]{2,1,0:T(8,128)(2,1)} all-to-all(bf16[64,8,2176]{2,1,0:T(8,128)(2,1)} %shard_map.175), channel_id=1, replica_groups=mesh['xh'=2,'y'=4,'core'=2,'z'=4,'dp'=2] {'dp','xh','y','z'}, dimensions={0} | all-to-all | bytes 4456448 | tf_op jit(solution)/shard_map/all_to_all | solution.py:471
  241.2 4.9 %shard_map.178 = bf16[32,8,4352]{2,1,0:T(8,128)(2,1)} custom-call(bf16[64,8,2176]{2,1,0:T(8,128)(2,1)} %all_to_all.15.pieces0, bf16[64,8,2176]{2,1,0:T(8,128)(2,1)} %copy-done.1), custom_call_target="tpu_custom_call" | custom-call | flops 5000000 | bytes 4000000 | tf_op jit(solution)/shard_map/pallas_call | solution.py:527
  246.1 34.8 %all_to_all.16.whole.whole0.whole1 = bf16[32,8,4352]{2,1,0:T(8,128)(2,1)S(1)} all-to-all(bf16[32,8,4352]{2,1,0:T(8,128)(2,1)} %shard_map.178), channel_id=1, replica_groups=mesh['xh'=2,'y'=4,'core'=2,'z'=4,'dp'=2] {'xh','y','z'}, dimensions={0} | all-to-all | bytes 4456448 | tf_op jit(solution)/shard_map/all_to_all | solution.py:528
  280.9 2.5 collective-permute-start.26
  283.4 2.1 collective-permute-start.20
  285.5 2.2 collective-permute-start.21
  287.8 3.7 %collective-permute-done.21.bottom = bf16[96,512]{1,0:T(8,128)(2,1)S(1)} collective-permute-done((bf16[96,512]{1,0:T(8,128)(2,1)S(1)}, bf16[96,512]{1,0:T(8,128)(2,1)S(1)}, u32[]{:S(2)}, u32[]{:S(2)}) %collective-permute-start.21) | collective-permute-done | bytes 98336 | tf_op jit(solution)/shard_map/ppermute | solution.py:438
  292.1 3.3 %shard_map.172 = (f32[4480,128]{1,0:T(8,128)}, bf16[336,128]{1,0:T(8,128)(2,1)}, bf16[336,128]{1,0:T(8,128)(2,1)}) custom-call(f32[4480,128]{1,0:T(8,128)} %get-tuple-element.96.old.grads, bf16[96,512]{1,0:T(8,128)(2,1)} %copy-done.17, bf16[96,512]{1,0:T(8,128)(2,1)} %copy-done.19), custom_call_target="tpu_custom_call" | custom-call | flops 10000000 | bytes 4000000 | tf_op jit(solution)/shard_map/pallas_call | solution.py:341
  295.4 2.0 collective-permute-start.22
  299.3 3.6 %collective-permute-done.23.right = bf16[336,128]{1,0:T(8,128)(2,1)S(1)} collective-permute-done((bf16[336,128]{1,0:T(8,128)(2,1)}, bf16[336,128]{1,0:T(8,128)(2,1)S(1)}, u32[]{:S(2)}, u32[]{:S(2)}) %collective-permute-start.23) | collective-permute-done | bytes 86048 | tf_op jit(solution)/shard_map/ppermute | solution.py:444
  303.6 7.8 %shard_map.173 = bf16[512,512]{1,0:T(8,128)(2,1)} custom-call(f32[4480,128]{1,0:T(8,128)} %get-tuple-element.99.old, bf16[336,128]{1,0:T(8,128)(2,1)} %copy-done.24, bf16[336,128]{1,0:T(8,128)(2,1)} %copy-done.25, f32[392,128]{1,0:T(8,128)} %bitcast.41, f32[512,512]{1,0:T(8,128)} %shard_map.170.u), custom_call_target="tpu_custom_call" | custom-call | flops 40000000 | bytes 4000000 | tf_op jit(solution)/shard_map/pallas_call | solution.py:380
  311.4 1.7 shard_map.180
  313.1 1.8 copy.26
  316.3 6.2 %shard_map.179 = (f32[2,256,2048]{2,1,0:T(8,128)}, f32[2,2048,256]{2,1,0:T(8,128)}) custom-call(s32[2]{0:T(128)} %pad_add_fusion.place, bf16[32,8,4352]{2,1,0:T(8,128)(2,1)} %copy-done, bf16[32,8,4352]{2,1,0:T(8,128)(2,1)} %collective-permute-done.26.mate.mate0.mate1), custom_call_target="tpu_custom_call" | custom-call | flops 10000000 | bytes 12000000 | tf_op jit(solution)/shard_map/pallas_call | solution.py:392
  (133 shorter events, 30.0 us)
Async XLA Ops:
  0.6 14.9 %copy-start.2 = (bf16[2,256,2048]{2,1,0:T(8,128)(2,1)S(1)}, bf16[2,256,2048]{2,1,0:T(8,128)(2,1)}, u32[]{:S(2)}) copy-start(bf16[2,256,2048]{2,1,0:T(8,128)(2,1)} %param.17) | copy-start | bytes 6291460
  2.4 16.7 %collective-permute-start = (bf16[96,512]{1,0:T(8,128)(2,1)}, bf16[96,512]{1,0:T(8,128)(2,1)}, u32[]{:S(2)}, u32[]{:S(2)}) collective-permute-start(bf16[96,512]{1,0:T(8,128)(2,1)} %bitcast.3), channel_id=1, source_target_pairs={{0,8},{8,16},{16,24},{24,32},{32,40},{40,48},{48,56},{56,64},{64,7... | collective-permute-start | bytes 294920 | tf_op jit(solution)/shard_map/ppermute | solution.py:437
  7.0 12.1 %collective-permute-start.1 = (bf16[96,512]{1,0:T(8,128)(2,1)S(1)}, bf16[96,512]{1,0:T(8,128)(2,1)}, u32[]{:S(2)}, u32[]{:S(2)}) collective-permute-start(bf16[96,512]{1,0:T(8,128)(2,1)S(1)} %bitcast.47), channel_id=1, source_target_pairs={{8,0},{16,8},{24,16},{32,24},{40,32},{48,40},{56,48},{64,56},{72,6... | collective-permute-start | bytes 294920 | tf_op jit(solution)/shard_map/ppermute | solution.py:438
  10.8 20.4 %collective-permute-start.4 = (bf16[128,2048]{1,0:T(8,128)(2,1)}, bf16[128,2048]{1,0:T(8,128)(2,1)S(1)}, u32[]{:S(2)}, u32[]{:S(2)}) collective-permute-start(bf16[128,2048]{1,0:T(8,128)(2,1)} %dynamic-slice_bitcast_fusion.3), channel_id=1, source_target_pairs={{0,1},{1,64},{64,65},{65,0},{2,3},{3,66},{66,67},{67,2},{4,5},{5,6... | collective-permute-start | bytes 1572872 | tf_op jit(solution)/shard_map/ppermute | solution.py:453
  12.0 4.6 %copy-start.3 = (bf16[2,2048,256]{2,1,0:T(8,128)(2,1)S(1)}, bf16[2,2048,256]{2,1,0:T(8,128)(2,1)}, u32[]{:S(2)}) copy-start(bf16[2,2048,256]{2,1,0:T(8,128)(2,1)} %param.19) | copy-start | bytes 6291460
  14.0 3.8 %copy-start.32 = (f32[2,512]{1,0:T(2,128)S(1)}, f32[2,512]{1,0:T(2,128)}, u32[]{:S(2)}) copy-start(f32[2,512]{1,0:T(2,128)} %param.16) | copy-start | bytes 12292
  14.0 3.8 %copy-start.33 = (f32[2,512]{1,0:T(2,128)S(1)}, f32[2,512]{1,0:T(2,128)}, u32[]{:S(2)}) copy-start(f32[2,512]{1,0:T(2,128)} %param.14) | copy-start | bytes 12292
  14.0 4.4 %copy-start.34 = (f32[2,512]{1,0:T(2,128)S(1)}, f32[2,512]{1,0:T(2,128)}, u32[]{:S(2)}) copy-start(f32[2,512]{1,0:T(2,128)} %param.21) | copy-start | bytes 12292
  14.0 4.4 %copy-start.35 = (f32[2,512]{1,0:T(2,128)S(1)}, f32[2,512]{1,0:T(2,128)}, u32[]{:S(2)}) copy-start(f32[2,512]{1,0:T(2,128)} %param.20) | copy-start | bytes 12292
  14.0 22.8 %collective-permute-start.6 = (bf16[1024,256]{1,0:T(8,128)(2,1)}, bf16[1024,256]{1,0:T(8,128)(2,1)S(1)}, u32[]{:S(2)}, u32[]{:S(2)}) collective-permute-start(bf16[1024,256]{1,0:T(8,128)(2,1)} %dynamic-slice_bitcast_fusion.2), channel_id=1, source_target_pairs={{0,65},{1,0},{64,1},{65,64},{2,67},{3,2},{66,3},{67,66},{4,69},{5,... | collective-permute-start | bytes 1572872 | tf_op jit(solution)/shard_map/ppermute | solution.py:453
  16.6 8.8 %copy-start.31 = (f32[2,512]{1,0:T(2,128)S(1)}, f32[2,512]{1,0:T(2,128)}, u32[]{:S(2)}) copy-start(f32[2,512]{1,0:T(2,128)} %param.15) | copy-start | bytes 12292
  17.7 19.2 %copy-start.30 = (f32[2,2048]{1,0:T(2,128)S(1)}, f32[2,2048]{1,0:T(2,128)}, u32[]{:S(2)}) copy-start(f32[2,2048]{1,0:T(2,128)} %param.18) | copy-start | bytes 49156
  21.9 5.4 %collective-permute-start.2 = (bf16[336,128]{1,0:T(8,128)(2,1)}, bf16[336,128]{1,0:T(8,128)(2,1)S(1)}, u32[]{:S(2)}, u32[]{:S(2)}) collective-permute-start(bf16[336,128]{1,0:T(8,128)(2,1)} %get-tuple-element.63), channel_id=1, source_target_pairs={{0,2},{2,4},{4,6},{1,3},{3,5},{5,7},{8,10},{10,12},{12,14},{9,11},... | collective-permute-start | bytes 258056 | tf_op jit(solution)/shard_map/ppermute | solution.py:443
  26.0 11.6 %copy-start.38 = (bf16[336,128]{1,0:T(8,128)(2,1)S(1)}, bf16[336,128]{1,0:T(8,128)(2,1)}, u32[]{:S(2)}) copy-start(bf16[336,128]{1,0:T(8,128)(2,1)} %get-tuple-element.64) | copy-start | bytes 258052
  27.2 17.6 %copy-start.26 = (bf16[336,128]{1,0:T(8,128)(2,1)}, bf16[336,128]{1,0:T(8,128)(2,1)S(1)}, u32[]{:S(2)}) copy-start(bf16[336,128]{1,0:T(8,128)(2,1)S(1)} %collective-permute-done.2.left) | copy-start | bytes 258052
  27.3 26.7 %collective-permute-start.12 = (bf16[128,2048]{1,0:T(8,128)(2,1)S(1)}, bf16[128,2048]{1,0:T(8,128)(2,1)S(1)}, u32[]{:S(2)}, u32[]{:S(2)}) collective-permute-start(bf16[128,2048]{1,0:T(8,128)(2,1)S(1)} %dynamic-slice_bitcast_fusion.1), channel_id=1, source_target_pairs={{0,1},{1,64},{64,65},{65,0},{2,3},{3,66},{66,67},{67,2},{4,5},{5,6... | collective-permute-start | bytes 1572872 | tf_op jit(solution)/shard_map/ppermute | solution.py:453
  28.4 26.5 %collective-permute-start.14 = (bf16[1024,256]{1,0:T(8,128)(2,1)S(1)}, bf16[1024,256]{1,0:T(8,128)(2,1)S(1)}, u32[]{:S(2)}, u32[]{:S(2)}) collective-permute-start(bf16[1024,256]{1,0:T(8,128)(2,1)S(1)} %dynamic-slice_bitcast_fusion), channel_id=1, source_target_pairs={{0,65},{1,0},{64,1},{65,64},{2,67},{3,2},{66,3},{67,66},{4,69},{5,... | collective-permute-start | bytes 1572872 | tf_op jit(solution)/shard_map/ppermute | solution.py:453
  31.2 23.9 %copy-start.9 = (bf16[128,2048]{1,0:T(8,128)(2,1)}, bf16[128,2048]{1,0:T(8,128)(2,1)S(1)}, u32[]{:S(2)}) copy-start(bf16[128,2048]{1,0:T(8,128)(2,1)S(1)} %collective-permute-done.4.got_in) | copy-start | bytes 1572868
  31.2 23.9 %collective-permute-start.5 = (bf16[128,2048]{1,0:T(8,128)(2,1)S(1)}, bf16[128,2048]{1,0:T(8,128)(2,1)S(1)}, u32[]{:S(2)}, u32[]{:S(2)}) collective-permute-start(bf16[128,2048]{1,0:T(8,128)(2,1)S(1)} %collective-permute-done.4.got_in), channel_id=1, source_target_pairs={{0,8},{8,0},{1,9},{9,1},{2,10},{10,2},{3,11},{11,3},{4,12},{12,4},... | collective-permute-start | bytes 1572872 | tf_op jit(solution)/shard_map/ppermute | solution.py:449
  36.8 18.3 %copy-start.10 = (bf16[1024,256]{1,0:T(8,128)(2,1)}, bf16[1024,256]{1,0:T(8,128)(2,1)S(1)}, u32[]{:S(2)}) copy-start(bf16[1024,256]{1,0:T(8,128)(2,1)S(1)} %collective-permute-done.6.got_out) | copy-start | bytes 1572868
  36.8 18.2 %collective-permute-start.7 = (bf16[1024,256]{1,0:T(8,128)(2,1)S(1)}, bf16[1024,256]{1,0:T(8,128)(2,1)S(1)}, u32[]{:S(2)}, u32[]{:S(2)}) collective-permute-start(bf16[1024,256]{1,0:T(8,128)(2,1)S(1)} %collective-permute-done.6.got_out), channel_id=1, source_target_pairs={{0,8},{8,0},{1,9},{9,1},{2,10},{10,2},{3,11},{11,3},{4,12},{12,4},... | collective-permute-start | bytes 1572872 | tf_op jit(solution)/shard_map/ppermute | solution.py:449
  37.6 6.4 %collective-permute-start.3 = (bf16[336,128]{1,0:T(8,128)(2,1)S(1)}, bf16[336,128]{1,0:T(8,128)(2,1)S(1)}, u32[]{:S(2)}, u32[]{:S(2)}) collective-permute-start(bf16[336,128]{1,0:T(8,128)(2,1)S(1)} %copy-done.38), channel_id=1, source_target_pairs={{2,0},{4,2},{6,4},{3,1},{5,3},{7,5},{10,8},{12,10},{14,12},{11,9},... | collective-permute-start | bytes 258056 | tf_op jit(solution)/shard_map/ppermute | solution.py:444
  53.9 12.6 %copy-start.7 = (bf16[128,2048]{1,0:T(8,128)(2,1)}, bf16[128,2048]{1,0:T(8,128)(2,1)S(1)}, u32[]{:S(2)}) copy-start(bf16[128,2048]{1,0:T(8,128)(2,1)S(1)} %collective-permute-done.12.got_in) | copy-start | bytes 1572868
  53.9 43.0 %collective-permute-start.13 = (bf16[128,2048]{1,0:T(8,128)(2,1)S(1)}, bf16[128,2048]{1,0:T(8,128)(2,1)S(1)}, u32[]{:S(2)}, u32[]{:S(2)}) collective-permute-start(bf16[128,2048]{1,0:T(8,128)(2,1)S(1)} %collective-permute-done.12.got_in), channel_id=1, source_target_pairs={{0,8},{8,0},{1,9},{9,1},{2,10},{10,2},{3,11},{11,3},{4,12},{12,4},... | collective-permute-start | bytes 1572872 | tf_op jit(solution)/shard_map/ppermute | solution.py:449
  54.9 11.6 %copy-start.8 = (bf16[1024,256]{1,0:T(8,128)(2,1)}, bf16[1024,256]{1,0:T(8,128)(2,1)S(1)}, u32[]{:S(2)}) copy-start(bf16[1024,256]{1,0:T(8,128)(2,1)S(1)} %collective-permute-done.14.got_out) | copy-start | bytes 1572868
  54.9 42.0 %collective-permute-start.15 = (bf16[1024,256]{1,0:T(8,128)(2,1)S(1)}, bf16[1024,256]{1,0:T(8,128)(2,1)S(1)}, u32[]{:S(2)}, u32[]{:S(2)}) collective-permute-start(bf16[1024,256]{1,0:T(8,128)(2,1)S(1)} %collective-permute-done.14.got_out), channel_id=1, source_target_pairs={{0,8},{8,0},{1,9},{9,1},{2,10},{10,2},{3,11},{11,3},{4,12},{12,4},... | collective-permute-start | bytes 1572872 | tf_op jit(solution)/shard_map/ppermute | solution.py:449
  66.6 16.6 %copy-start.4 = (bf16[2,2048,256]{2,1,0:T(8,128)(2,1)S(1)}, bf16[2,2048,256]{2,1,0:T(8,128)(2,1)}, u32[]{:S(2)}) copy-start(bf16[2,2048,256]{2,1,0:T(8,128)(2,1)} %param.19) | copy-start | bytes 6291460
  66.6 5.5 %collective-permute-start.8 = (bf16[96,512]{1,0:T(8,128)(2,1)}, bf16[96,512]{1,0:T(8,128)(2,1)S(1)}, u32[]{:S(2)}, u32[]{:S(2)}) collective-permute-start(bf16[96,512]{1,0:T(8,128)(2,1)} %get-tuple-element.67), channel_id=1, source_target_pairs={{0,8},{8,16},{16,24},{24,32},{32,40},{40,48},{48,56},{56,64},{64,7... | collective-permute-start | bytes 294920 | tf_op jit(solution)/shard_map/ppermute | solution.py:437
  68.6 6.1 %collective-permute-start.9 = (bf16[96,512]{1,0:T(8,128)(2,1)}, bf16[96,512]{1,0:T(8,128)(2,1)S(1)}, u32[]{:S(2)}, u32[]{:S(2)}) collective-permute-start(bf16[96,512]{1,0:T(8,128)(2,1)} %get-tuple-element.68), channel_id=1, source_target_pairs={{8,0},{16,8},{24,16},{32,24},{40,32},{48,40},{56,48},{64,56},{72,6... | collective-permute-start | bytes 294920 | tf_op jit(solution)/shard_map/ppermute | solution.py:438
  78.2 6.1 %collective-permute-start.10 = (bf16[336,128]{1,0:T(8,128)(2,1)}, bf16[336,128]{1,0:T(8,128)(2,1)S(1)}, u32[]{:S(2)}, u32[]{:S(2)}) collective-permute-start(bf16[336,128]{1,0:T(8,128)(2,1)} %get-tuple-element.70), channel_id=1, source_target_pairs={{0,2},{2,4},{4,6},{1,3},{3,5},{5,7},{8,10},{10,12},{12,14},{9,11},... | collective-permute-start | bytes 258056 | tf_op jit(solution)/shard_map/ppermute | solution.py:443
  81.7 5.4 %collective-permute-start.11 = (bf16[336,128]{1,0:T(8,128)(2,1)}, bf16[336,128]{1,0:T(8,128)(2,1)S(1)}, u32[]{:S(2)}, u32[]{:S(2)}) collective-permute-start(bf16[336,128]{1,0:T(8,128)(2,1)} %get-tuple-element.71), channel_id=1, source_target_pairs={{2,0},{4,2},{6,4},{3,1},{5,3},{7,5},{10,8},{12,10},{14,12},{11,9},... | collective-permute-start | bytes 258056 | tf_op jit(solution)/shard_map/ppermute | solution.py:444
  119.8 23.6 %collective-permute-start.25 = (bf16[512,2048]{1,0:T(8,128)(2,1)}, bf16[512,2048]{1,0:T(8,128)(2,1)S(1)}, u32[]{:S(2)}, u32[]{:S(2)}) collective-permute-start(bf16[512,2048]{1,0:T(8,128)(2,1)} %get-tuple-element.108), channel_id=1, source_target_pairs={{0,8},{8,0},{1,9},{9,1},{2,10},{10,2},{3,11},{11,3},{4,12},{12,4},... | collective-permute-start | bytes 6291464 | tf_op jit(solution)/shard_map/ppermute | solution.py:449
  119.8 14.3 %collective-permute-start.16 = (bf16[96,512]{1,0:T(8,128)(2,1)}, bf16[96,512]{1,0:T(8,128)(2,1)S(1)}, u32[]{:S(2)}, u32[]{:S(2)}) collective-permute-start(bf16[96,512]{1,0:T(8,128)(2,1)} %get-tuple-element.84), channel_id=1, source_target_pairs={{0,8},{8,16},{16,24},{24,32},{32,40},{40,48},{48,56},{56,64},{64,7... | collective-permute-start | bytes 294920 | tf_op jit(solution)/shard_map/ppermute | solution.py:437
  123.2 10.9 %collective-permute-start.17 = (bf16[96,512]{1,0:T(8,128)(2,1)}, bf16[96,512]{1,0:T(8,128)(2,1)S(1)}, u32[]{:S(2)}, u32[]{:S(2)}) collective-permute-start(bf16[96,512]{1,0:T(8,128)(2,1)} %get-tuple-element.85), channel_id=1, source_target_pairs={{8,0},{16,8},{24,16},{32,24},{40,32},{48,40},{56,48},{64,56},{72,6... | collective-permute-start | bytes 294920 | tf_op jit(solution)/shard_map/ppermute | solution.py:438
  138.7 22.0 %collective-permute-start.18 = (bf16[336,128]{1,0:T(8,128)(2,1)}, bf16[336,128]{1,0:T(8,128)(2,1)S(1)}, u32[]{:S(2)}, u32[]{:S(2)}) collective-permute-start(bf16[336,128]{1,0:T(8,128)(2,1)} %get-tuple-element.87), channel_id=1, source_target_pairs={{0,2},{2,4},{4,6},{1,3},{3,5},{5,7},{8,10},{10,12},{12,14},{9,11},... | collective-permute-start | bytes 258056 | tf_op jit(solution)/shard_map/ppermute | solution.py:443
  142.1 18.7 %collective-permute-start.19 = (bf16[336,128]{1,0:T(8,128)(2,1)}, bf16[336,128]{1,0:T(8,128)(2,1)S(1)}, u32[]{:S(2)}, u32[]{:S(2)}) collective-permute-start(bf16[336,128]{1,0:T(8,128)(2,1)} %get-tuple-element.88), channel_id=1, source_target_pairs={{2,0},{4,2},{6,4},{3,1},{5,3},{7,5},{10,8},{12,10},{14,12},{11,9},... | collective-permute-start | bytes 258056 | tf_op jit(solution)/shard_map/ppermute | solution.py:444
  148.9 50.0 %all-to-all-start.1 = ((bf16[64,8,2176]{2,1,0:T(8,128)(2,1)}), bf16[64,8,2176]{2,1,0:T(8,128)(2,1)S(1)}, u32[]{:S(2)}, u32[]{:S(2)}) async-start(bf16[64,8,2176]{2,1,0:T(8,128)(2,1)} %shard_map.177), calls=%async_computation.1 | async-start | bytes 4456448 | tf_op jit(solution)/shard_map/all_to_all | solution.py:471
  180.8 12.5 %collective-permute-start.24 = (bf16[512,2048]{1,0:T(8,128)(2,1)}, bf16[512,2048]{1,0:T(8,128)(2,1)S(1)}, u32[]{:S(2)}, u32[]{:S(2)}) collective-permute-start(bf16[512,2048]{1,0:T(8,128)(2,1)} %get-tuple-element.103), channel_id=1, source_target_pairs={{0,8},{8,0},{1,9},{9,1},{2,10},{10,2},{3,11},{11,3},{4,12},{12,4},... | collective-permute-start | bytes 6291464 | tf_op jit(solution)/shard_map/ppermute | solution.py:449
  198.9 42.3 %copy-start.1 = (bf16[64,8,2176]{2,1,0:T(8,128)(2,1)}, bf16[64,8,2176]{2,1,0:T(8,128)(2,1)S(1)}, u32[]{:S(2)}) copy-start(bf16[64,8,2176]{2,1,0:T(8,128)(2,1)S(1)} %all-to-all-done.1.pieces1) | copy-start | bytes 6684676
  246.1 37.3 %copy-start.37 = (bf16[96,512]{1,0:T(8,128)(2,1)S(1)}, bf16[96,512]{1,0:T(8,128)(2,1)}, u32[]{:S(2)}) copy-start(bf16[96,512]{1,0:T(8,128)(2,1)} %get-tuple-element.97) | copy-start | bytes 294916
  246.1 39.4 %copy-start.36 = (bf16[96,512]{1,0:T(8,128)(2,1)S(1)}, bf16[96,512]{1,0:T(8,128)(2,1)}, u32[]{:S(2)}) copy-start(bf16[96,512]{1,0:T(8,128)(2,1)} %get-tuple-element.98) | copy-start | bytes 294916
  280.9 30.5 %copy-start = (bf16[32,8,4352]{2,1,0:T(8,128)(2,1)}, bf16[32,8,4352]{2,1,0:T(8,128)(2,1)S(1)}, u32[]{:S(2)}) copy-start(bf16[32,8,4352]{2,1,0:T(8,128)(2,1)S(1)} %all_to_all.16.whole.whole0.whole1) | copy-start | bytes 6684676
  280.9 30.5 %collective-permute-start.26 = (bf16[32,8,4352]{2,1,0:T(8,128)(2,1)S(1)}, bf16[32,8,4352]{2,1,0:T(8,128)(2,1)}, u32[]{:S(2)}, u32[]{:S(2)}) collective-permute-start(bf16[32,8,4352]{2,1,0:T(8,128)(2,1)S(1)} %all_to_all.16.whole.whole0.whole1), channel_id=1, source_target_pairs={{0,8},{8,0},{1,9},{9,1},{2,10},{10,2},{3,11},{11,3},{4,12},{12,4},... | collective-permute-start | bytes 6684680 | tf_op jit(solution)/shard_map/ppermute | solution.py:449
  283.4 4.3 %collective-permute-start.20 = (bf16[96,512]{1,0:T(8,128)(2,1)S(1)}, bf16[96,512]{1,0:T(8,128)(2,1)S(1)}, u32[]{:S(2)}, u32[]{:S(2)}) collective-permute-start(bf16[96,512]{1,0:T(8,128)(2,1)S(1)} %copy-done.37), channel_id=1, source_target_pairs={{0,8},{8,16},{16,24},{24,32},{32,40},{40,48},{48,56},{56,64},{64,7... | collective-permute-start | bytes 294920 | tf_op jit(solution)/shard_map/ppermute | solution.py:437
  285.5 5.9 %collective-permute-start.21 = (bf16[96,512]{1,0:T(8,128)(2,1)S(1)}, bf16[96,512]{1,0:T(8,128)(2,1)S(1)}, u32[]{:S(2)}, u32[]{:S(2)}) collective-permute-start(bf16[96,512]{1,0:T(8,128)(2,1)S(1)} %copy-done.36), channel_id=1, source_target_pairs={{8,0},{16,8},{24,16},{32,24},{40,32},{48,40},{56,48},{64,56},{72,6... | collective-permute-start | bytes 294920 | tf_op jit(solution)/shard_map/ppermute | solution.py:438
  295.4 3.9 %collective-permute-start.22 = (bf16[336,128]{1,0:T(8,128)(2,1)}, bf16[336,128]{1,0:T(8,128)(2,1)S(1)}, u32[]{:S(2)}, u32[]{:S(2)}) collective-permute-start(bf16[336,128]{1,0:T(8,128)(2,1)} %get-tuple-element.100), channel_id=1, source_target_pairs={{0,2},{2,4},{4,6},{1,3},{3,5},{5,7},{8,10},{10,12},{12,14},{9,11},... | collective-permute-start | bytes 258056 | tf_op jit(solution)/shard_map/ppermute | solution.py:443
  297.5 5.4 %collective-permute-start.23 = (bf16[336,128]{1,0:T(8,128)(2,1)}, bf16[336,128]{1,0:T(8,128)(2,1)S(1)}, u32[]{:S(2)}, u32[]{:S(2)}) collective-permute-start(bf16[336,128]{1,0:T(8,128)(2,1)} %get-tuple-element.101), channel_id=1, source_target_pairs={{2,0},{4,2},{6,4},{3,1},{5,3},{7,5},{10,8},{12,10},{14,12},{11,9},... | collective-permute-start | bytes 258056 | tf_op jit(solution)/shard_map/ppermute | solution.py:444
  299.3 4.3 %copy-start.24 = (bf16[336,128]{1,0:T(8,128)(2,1)}, bf16[336,128]{1,0:T(8,128)(2,1)S(1)}, u32[]{:S(2)}) copy-start(bf16[336,128]{1,0:T(8,128)(2,1)S(1)} %collective-permute-done.22.left) | copy-start | bytes 258052
  (19 other events, 26.2 us)
where the time goes:
time: 327 us; the launch traced here: 322 us
  Pallas kernels  129 us (39%)
  blocking collectives  77.1 us (24%)
  starting transfers between devices  68.4 us (21%)
  local copies, waits for them, and re-layouts  27.3 us (8%)
  waiting for transfers between devices  19 us (6%)
    all_to_all x1, blocking collectives, send_grads(): return lax.all_to_all(pair, ('dp', *SPACE), 0, 0, tiled=True)  42.3 us
    all_to_all x1, blocking collectives, per_device(): whole = lax.all_to_all(copies, SPACE, 0, 0, tiled=True)  34.8 us
    pallas_call x2, Pallas kernels, backward(): call(back_body, outs, 12, 100000000, scratch, scalars=1)  23 us
    pallas_call x2, Pallas kernels, mlp(): call(mlp_body, outs, 12, 60000000, scalars=1)  20.9 us
    pallas_call x2, Pallas kernels, normalise(): call(norm_body, outs, 7, 40000000, [STORE])  18.1 us
    pallas_call x2, Pallas kernels, tap_grads(): return call(taps_body, [((49 * 4, 128), F32)], 2, 40000000)(seen, grads)[0]  18 us
    pallas_call x2, Pallas kernels, upstream(): call(up_body, [((PIX, CH), dtype)], 5, 40000000, scratch)  15.5 us
    ppermute x7, starting transfers between devices, swapped(): return lax.ppermute(value, axis, [(0, 1), (1, 0)])  12.9 us
  transfers between devices with their start and end apart: 28, of which 7 were waited for; matrix products, arithmetic and copies ran while one was open for 5% of the time, Pallas kernels for 29%

commit v1 on v0

--- a/solution.py
+++ b/solution.py
@@ -1,3 +1,5 @@
+import functools
+
 import jax
 import jax.numpy as jnp
 from jax import lax
@@ -25,7 +27,7 @@
 SM = pl.BlockSpec(memory_space=pltpu.SMEM)
 
 
-def call(body, outs, count, flops, scratch=(), scalars=0):
+def call(body, outs, count, flops, scratch=(), scalars=0, grant=12):
     shapes = [jax.ShapeDtypeStruct(s, d) for s, d in outs]
     return pl.pallas_call(
         body,
@@ -33,7 +35,7 @@
         in_specs=[SM] * scalars + [VM] * (count - scalars),
         out_specs=[VM] * len(outs),
         scratch_shapes=list(scratch),
-        compiler_params=pltpu.CompilerParams(vmem_limit_bytes=56 * 1024 * 1024),
+        compiler_params=pltpu.CompilerParams(vmem_limit_bytes=grant * 1024 * 1024),
         cost_estimate=pl.CostEstimate(
             flops=flops, bytes_accessed=4_000_000, transcendentals=0
         ),
@@ -81,7 +83,17 @@
         to_high[a:b, :] = slab[pl.ds(at(row, 32), 24), :].astype(BF16)
 
 
-def filtered(slab, taps, store):
+def spread(kernel, k, taps):
+    for tap in range(49):
+        line = kernel[tap // 7, tap % 7, k : k + 1, :]
+        for part in range(8):
+            group = part % 4
+            taps[tap * 8 + part : tap * 8 + part + 1, :] = line[
+                :, group * 128 : (group + 1) * 128
+            ]
+
+
+def filtered(slab, taps, store, turned):
     def step(n, carry):
         row = n // 4
         col = (n % 4) * 8
@@ -90,7 +102,8 @@
             base = pl.multiple_of(((row + p) * WIDE + col) * 8, 8)
             seen = [slab[pl.ds(base + 8 * k, 8), :] for k in range(14)]
             for q in range(7):
-                weight = taps[(p * 7 + q) * 8 : (p * 7 + q + 1) * 8, :]
+                tap = 48 - p * 7 - q if turned else p * 7 + q
+                weight = taps[tap * 8 : tap * 8 + 8, :]
                 for m in range(8):
                     term = seen[m + q] * weight
                     sums[m] = term if sums[m] is None else sums[m] + term
@@ -126,39 +139,44 @@
     take_columns(slab, to_low, to_high)
 
 
-def norm_body(old, left, right, taps, bias, gain, shift, slab, normal, normed, rstd, store):
+def norm_body(
+    k, old, left, right, kernel, bias, gain, shift, slab, normal, normed, rstd, store, taps
+):
+    one = slice(k, k + 1)
+    spread(kernel, k, taps)
     slab[...] = old[...]
     put_columns(slab, left, right)
-    filtered(slab, taps, store)
+    filtered(slab, taps, store, False)
     for row in range(ROWS):
         a, b = row * COLS, (row + 1) * COLS
-        mixed = line_of(store, row) + bias[...]
+        mixed = line_of(store, row) + bias[one, :]
         center = mixed - jnp.mean(mixed, -1, keepdims=True)
         scale = lax.rsqrt(jnp.mean(center * center, -1, keepdims=True) + EPSILON)
         value = center * scale
         normed[a:b, :] = value
         rstd[a:b, :] = jnp.broadcast_to(scale, (COLS, 128))
-        normal[a:b, :] = (value * gain[...] + shift[...]).astype(BF16)
+        normal[a:b, :] = (value * gain[one, :] + shift[one, :]).astype(BF16)
 
 
 def mlp_body(
-    place, a, normal, own_in, got_in, mate_in, own_out, got_out, mate_out,
+    k, place, a, normal, own_in, got_in, mate_in, own_out, got_out, mate_out,
     bias_in, bias_out, scale,
     out, top, bottom, act, slope, branch, full_in, full_out,
 ):
+    one = slice(k, k + 1)
     core, part = place[0], place[1]
     mine = pl.multiple_of(part * 256, 256)
     theirs = pl.multiple_of((1 - part) * 256, 256)
-    full_in[pl.ds(mine, 256), :] = own_in[...]
+    full_in[pl.ds(mine, 256), :] = own_in[k]
     full_in[pl.ds(pl.multiple_of(theirs + core * 128, 128), 128), :] = got_in[...]
     full_in[pl.ds(pl.multiple_of(theirs + (1 - core) * 128, 128), 128), :] = mate_in[...]
-    full_out[:, pl.ds(mine, 256)] = own_out[...]
+    full_out[:, pl.ds(mine, 256)] = own_out[k]
     full_out[pl.ds(pl.multiple_of(core * HALF, HALF), HALF), pl.ds(theirs, 256)] = got_out[...]
     full_out[pl.ds(pl.multiple_of((1 - core) * HALF, HALF), HALF), pl.ds(theirs, 256)] = mate_out[...]
     for c in range(8):
         cols = slice(c * 256, (c + 1) * 256)
         hidden = jnp.dot(normal[...], full_in[:, cols], preferred_element_type=F32)
-        v = hidden + bias_in[:, cols]
+        v = hidden + bias_in[one, cols]
         square = v * v
         tangent = jnp.tanh(v * (COEF + (COEF * CUBIC) * square))
         half = 0.5 * v
@@ -171,24 +189,23 @@
     for c in range(2):
         cols = slice(c * 256, (c + 1) * 256)
         value = jnp.dot(act[...], full_out[:, cols], preferred_element_type=F32)
-        value = value + bias_out[:, cols]
+        value = value + bias_out[one, cols]
         branch[:, cols] = value
-        result = (a[:, cols].astype(F32) + scale[:, cols] * value).astype(BF16)
+        result = (a[:, cols].astype(F32) + scale[one, cols] * value).astype(BF16)
         out[:, cols] = result
         top[:, cols] = result[:96, :]
         bottom[:, cols] = result[416:, :]
 
 
 def back_body(
-    place, u, branch, act, slope, normal, normed, rstd, full_in, full_out, gain, scale,
-    keep, give, slab, top, bottom, channel, bias, low, gh, gn,
+    k, u, branch, slope, normed, rstd, full_in, full_out, gain, scale,
+    low, gh, slab, top, bottom, channel, bias, gn,
 ):
-    core = place[0]
-    rows_first = (((0,), (0,)), ((), ()))
+    one = slice(k, k + 1)
     cols_last = (((1,), (1,)), ((), ()))
     up = u[...].astype(F32)
     channel[4:5, :] = jnp.sum(up * branch[...], 0, keepdims=True)
-    gb = up * scale[...]
+    gb = up * scale[one, :]
     channel[3:4, :] = jnp.sum(gb, 0, keepdims=True)
     low[...] = gb.astype(BF16)
     for c in range(8):
@@ -199,15 +216,6 @@
         value = ga * slope[:, cols].astype(F32)
         bias[:, cols] = jnp.sum(value, 0, keepdims=True)
         gh[:, cols] = value.astype(BF16)
-    for side, ref in ((core, keep), (1 - core, give)):
-        for c in range(4):
-            cols = pl.ds(pl.multiple_of(side * HALF + c * 256, 256), 256)
-            ref[:, c * 256 : (c + 1) * 256] = lax.dot_general(
-                normal[...], gh[:, cols], rows_first, preferred_element_type=F32
-            ).astype(BF16)
-            ref[:, HALF + c * 256 : HALF + (c + 1) * 256] = lax.dot_general(
-                low[...], act[:, cols], rows_first, preferred_element_type=F32
-            ).astype(BF16)
     for c in range(2):
         cols = slice(c * 256, (c + 1) * 256)
         gn[:, cols] = lax.dot_general(
@@ -224,7 +232,7 @@
         value = normed[a:b, :]
         sums[1] += folded(grad * value)
         sums[2] += folded(grad)
-        gs = grad * gain[...]
+        gs = grad * gain[one, :]
         gm = rstd[a:b, 0:1] * (
             gs
             - jnp.mean(gs, -1, keepdims=True)
@@ -236,8 +244,22 @@
             top[a:b, :] = gm.astype(BF16)
         if row >= 13:
             bottom[a - 416 : b - 416, :] = gm.astype(BF16)
-    for k in range(3):
-        channel[k : k + 1, :] = jnp.sum(sums[k], 0, keepdims=True)
+    for n in range(3):
+        channel[n : n + 1, :] = jnp.sum(sums[n], 0, keepdims=True)
+
+
+def grads_body(place, normal, low, act, gh, keep, give):
+    core = place[0]
+    rows_first = (((0,), (0,)), ((), ()))
+    for side, ref in ((1 - core, give), (core, keep)):
+        for c in range(4):
+            cols = pl.ds(pl.multiple_of(side * HALF + c * 256, 256), 256)
+            ref[:, c * 256 : (c + 1) * 256] = lax.dot_general(
+                normal[...], gh[:, cols], rows_first, preferred_element_type=F32
+            ).astype(BF16)
+            ref[:, HALF + c * 256 : HALF + (c + 1) * 256] = lax.dot_general(
+                low[...], act[:, cols], rows_first, preferred_element_type=F32
+            ).astype(BF16)
 
 
 def taps_body(seen, grads, out):
@@ -261,10 +283,11 @@
             out[(p * 7 + q) * 4 : (p * 7 + q + 1) * 4, :] = sums[q][0:4] + sums[q][4:8]
 
 
-def up_body(old, left, right, taps, u, out, slab, store):
+def up_body(k, old, left, right, kernel, u, out, slab, store, taps):
+    spread(kernel, k, taps)
     slab[...] = old[...]
     put_columns(slab, left, right)
-    filtered(slab, taps, store)
+    filtered(slab, taps, store, True)
     for row in range(ROWS):
         a, b = row * COLS, (row + 1) * COLS
         out[a:b, :] = (u[a:b, :].astype(F32) + line_of(store, row)).astype(out.dtype)
@@ -313,8 +336,12 @@
         lines[0:256, :] = (whole[...].astype(F32) + mate[...].astype(F32)).reshape(256, 128)
         for group in range(4):
             cols = slice(group * 128, (group + 1) * 128)
-            taps[k, :, cols] = lines[pl.ds(group, 49, stride=4), :]
-            channel[k, :, cols] = lines[pl.ds(196 + group, 5, stride=4), :]
+            for tap in range(49):
+                line = tap * 4 + group
+                taps[tap // 7, tap % 7, k : k + 1, cols] = lines[line : line + 1, :]
+            for kind in range(5):
+                line = 196 + kind * 4 + group
+                channel[kind, k : k + 1, cols] = lines[line : line + 1, :]
         for group in range(16):
             bias[k : k + 1, group * 128 : (group + 1) * 128] = lines[216 + group : 217 + group, :]
 
@@ -329,6 +356,7 @@
 
 
 STORE = pltpu.VMEM((ROWS * COLS * 4 + 16, 128), F32)
+TAPS = pltpu.VMEM((400, 128), F32)
 STRIP = ((DEEP * 24, 128), BF16)
 EDGE = ((96, CH), BF16)
 
@@ -341,50 +369,48 @@
     return call(edge_body, [((SLAB, 128), F32), STRIP, STRIP], 3, 10_000_000)(slab, top, bottom)
 
 
-def normalise(slab, left, right, taps, bias, gain, shift):
+def normalise(k, slab, left, right, kernel, bias, gain, shift):
     outs = [((SLAB, 128), F32), ((PIX, CH), BF16), ((PIX, CH), F32), ((PIX, 128), F32)]
-    return call(norm_body, outs, 7, 40_000_000, [STORE])(
-        slab, left, right, taps, bias, gain, shift
-    )
-
-
-def mlp(place, a, normal, weights, bias_in, bias_out, scale):
+    return call(functools.partial(norm_body, k), outs, 7, 40_000_000, [STORE, TAPS])(
+        slab, left, right, kernel, bias, gain, shift
+    )
+
+
+def mlp(k, place, a, normal, weights, bias_in, bias_out, scale):
     outs = [
         ((PIX, CH), BF16), EDGE, EDGE, ((PIX, FF), BF16), ((PIX, FF), BF16),
         ((PIX, CH), F32), ((CH, FF), BF16), ((FF, CH), BF16),
     ]
-    return call(mlp_body, outs, 12, 60_000_000, scalars=1)(
+    return call(functools.partial(mlp_body, k), outs, 12, 60_000_000, scalars=1)(
         place, a, normal, *weights, bias_in, bias_out, scale
     )
 
 
-def backward(place, u, saved, gain, scale):
+def backward(k, u, saved, gain, scale):
     outs = [
-        ((CH, FF), BF16), ((CH, FF), BF16), ((SLAB, 128), F32), EDGE, EDGE,
+        ((PIX, CH), BF16), ((PIX, FF), BF16), ((SLAB, 128), F32), EDGE, EDGE,
         ((8, CH), F32), ((1, FF), F32),
     ]
-    scratch = [
-        pltpu.VMEM((PIX, CH), BF16), pltpu.VMEM((PIX, FF), BF16), pltpu.VMEM((PIX, CH), F32),
-    ]
-    return call(back_body, outs, 12, 100_000_000, scratch, scalars=1)(
-        place, u, *saved, gain, scale
-    )
+    scratch = [pltpu.VMEM((PIX, CH), F32)]
+    return call(functools.partial(back_body, k), outs, 9, 60_000_000, scratch)(
+        u, *saved, gain, scale
+    )
+
+
+def weight_grads(place, normal, low, act, gh):
+    outs = [((CH, FF), BF16), ((CH, FF), BF16)]
+    return call(grads_body, outs, 5, 50_000_000, scalars=1)(place, normal, low, act, gh)
 
 
 def tap_grads(seen, grads):
     return call(taps_body, [((49 * 4, 128), F32)], 2, 40_000_000)(seen, grads)[0]
 
 
-def upstream(slab, left, right, taps, u, dtype):
-    scratch = [pltpu.VMEM((SLAB, 128), F32), STORE]
-    return call(up_body, [((PIX, CH), dtype)], 5, 40_000_000, scratch)(
-        slab, left, right, taps, u
+def upstream(k, slab, left, right, kernel, u, dtype):
+    scratch = [pltpu.VMEM((SLAB, 128), F32), STORE, TAPS]
+    return call(functools.partial(up_body, k), [((PIX, CH), dtype)], 5, 40_000_000, scratch)(
+        slab, left, right, kernel, u
     )[0]
-
-
-def spread(taps):
-    lines = taps.reshape(49, 1, 4, 128)
-    return jnp.broadcast_to(lines, (49, 2, 4, 128)).reshape(49 * 8, 128)
 
 
 def finish(place, whole, mate):
@@ -410,15 +436,15 @@
 def finish_small(whole, mate):
     first = pl.BlockSpec((32, 8, 128), lambda i: (0, 0, FF // 128))
     second = pl.BlockSpec((32, 8, 128), lambda i: (0, 0, (WIRE + FF) // 128))
-    shapes = [(2, 49, CH), (2, 5, CH), (2, FF)]
+    shapes = [(7, 7, 2, CH), (5, 2, CH), (2, FF)]
     return pl.pallas_call(
         small_body,
         grid=(1,),
         out_shape=[jax.ShapeDtypeStruct(s, F32) for s in shapes],
         in_specs=[first, second, first, second],
         out_specs=[
-            pl.BlockSpec((2, 49, CH), lambda i: (0, 0, 0)),
-            pl.BlockSpec((2, 5, CH), lambda i: (0, 0, 0)),
+            pl.BlockSpec((7, 7, 2, CH), lambda i: (0, 0, 0, 0)),
+            pl.BlockSpec((5, 2, CH), lambda i: (0, 0, 0)),
             pl.BlockSpec((2, FF), lambda i: (0, 0)),
         ],
         scratch_shapes=[pltpu.VMEM((256 + 8, 128), F32)],
@@ -460,7 +486,7 @@
     got_out = around_x(half_out, -1)
     mate_in = swapped(got_in, "core")
     mate_out = swapped(got_out, "core")
-    return weight_in[k], got_in, mate_in, weight_out[k], got_out, mate_out
+    return got_in, mate_in, got_out, mate_out
 
 
 def send_grads(keep, got, taps, channel, bias):
@@ -486,44 +512,39 @@
 ):
     core, part = lax.axis_index("core"), lax.axis_index("dp")
     place = jnp.stack([core, part]).astype(jnp.int32)
-    one = lambda table, which: table[which][None]
+    kernel = jnp.transpose(kernel, (1, 2, 0, 3))
     current = slides.reshape(PIX, CH)
     top, bottom = current[:96], current[416:]
     saved = []
-    slabs = []
-    weights = fetch_weights(core, weight_in, weight_out, 0)
+    fetched = fetch_weights(core, weight_in, weight_out, 0)
     for k in range(2):
         above, below = from_rows(top, bottom)
         slab, to_low, to_high = pack(current, above, below)
         left, right = from_columns(to_low, to_high)
         slab, normal, normed, rstd = normalise(
-            slab, left, right, spread(kernel[k]),
-            one(kernel_bias, k), one(norm_gain, k), one(norm_bias, k),
+            k, slab, left, right, kernel, kernel_bias, norm_gain, norm_bias
         )
+        weights = (weight_in, *fetched[:2], weight_out, *fetched[2:])
         current, top, bottom, act, slope, branch, full_in, full_out = mlp(
-            place, current, normal, weights,
-            one(bias_in, k), one(bias_out, k), one(layer_scale, k),
+            k, place, current, normal, weights, bias_in, bias_out, layer_scale
         )
-        slabs.append(slab)
-        saved.append((branch, act, slope, normal, normed, rstd, full_in, full_out))
+        saved.append((slab, act, normal, (branch, slope, normed, rstd, full_in, full_out)))
         if k == 0:
-            later_in, later_out, _ = lax.optimization_barrier((weight_in, weight_out, left))
-            weights = fetch_weights(core, later_in, later_out, 1)
+            later_in, later_out, _ = lax.optimization_barrier((weight_in, weight_out, normal))
+            fetched = fetch_weights(core, later_in, later_out, 1)
     up = cotangent.reshape(PIX, CH)
     pieces = [None] * 2
     for k in (1, 0):
-        keep, give, grads, top, bottom, channel, bias = backward(
-            place, up, saved[k], one(norm_gain, k), one(layer_scale, k)
-        )
+        seen, act, normal, rest = saved[k]
+        low, gh, grads, top, bottom, channel, bias = backward(k, up, rest, norm_gain, layer_scale)
+        above, below = from_rows(top, bottom)
+        keep, give = weight_grads(place, normal, low, act, gh)
         got = swapped(give, "core")
-        above, below = from_rows(top, bottom)
-        taps = tap_grads(slabs[k], grads)
+        taps = tap_grads(seen, grads)
         pieces[k] = send_grads(keep, got, taps, channel, bias)
         slab, to_low, to_high = pack_edges(grads, above, below)
         left, right = from_columns(to_low, to_high)
-        up = upstream(
-            slab, left, right, spread(kernel[k][::-1, ::-1]), up, F32 if k else BF16
-        )
+        up = upstream(k, slab, left, right, kernel, up, F32 if k else BF16)
     copies = call(merge_body, [((32, 8, 2 * WIRE), BF16)], 2, 5_000_000)(*pieces)[0]
     whole = lax.all_to_all(copies, SPACE, 0, 0, tiled=True)
     mate = swapped(whole, "core")
@@ -534,8 +555,8 @@
         up.reshape(slides.shape),
         grad_in,
         grad_out,
-        grad_taps.reshape(2, 7, 7, CH),
-        grad_channel,
+        jnp.transpose(grad_taps, (2, 0, 1, 3)),
+        jnp.transpose(grad_channel, (1, 0, 2)),
         grad_bias,
     )
 

time: 327 us -> 285 us (0.87)
  Pallas kernels: 129 us -> 72.5 us
  starting transfers between devices: 68.4 us -> 75.1 us
  local copies, waits for them, and re-layouts: 27.3 us -> 32.1 us
  waiting for transfers between devices: 19 us -> 23.8 us
    pallas_call x8 -> x10, Pallas kernels: 77.6 us -> 46.1 us  [the longest x2 13.3 us: mlp(): call(functools.partial(mlp_body, k), outs, 12, 60000000, scalars=1)]
    unnamed x79 -> x100, local copies, waits for them, and re-layouts: 8.62 us -> 27.9 us
    pallas_call x2, Pallas kernels: 6.62 us -> 0.44 us  [pack_edges(): call(edge_body, [((SLAB, 128), F32), STRIP, STRIP], 3, 10000000)]
    pallas_call x2, Pallas kernels: 18 us -> 12.1 us  [tap_grads(): return call(taps_body, [((49 * 4, 128), F32)], 2, 40000000)(seen, grads)[0]]
    pallas_call x2, Pallas kernels: 8.37 us -> 2.52 us  [send_grads(): call(pair_body, [((64, 8, WIRE), BF16)], 5, 2000000, scratch)]
    ppermute x4, waiting for transfers between devices: 6.37 us -> 11.7 us  [from_rows(): below = lax.ppermute(top, RANKS, BACKWARD['rows'])]
    pallas_call x2, Pallas kernels: 5.52 us -> 0.55 us  [pack(): call(pack_body, [((SLAB, 128), F32), STRIP, STRIP], 3, 10000000)]
    squeeze x5 -> x0, local copies, waits for them, and re-layouts: 4.24 us -> none  [the longest x4 4.21 us: fetch_weights(): return (weight_in[k], got_in, mate_in, weight_out[k], got_out, mate_out)]
  transfers between devices with their start and end apart: 28 -> 28, of which waited for: 7 -> 9; matrix products, arithmetic and copies ran while one was open for 5% -> 1% of each run, Pallas kernels for 29% -> 17%
where the time goes in v1:
time: 285 us; the launch traced here: 280 us
  blocking collectives  75.5 us (26%)
  starting transfers between devices  75.1 us (26%)
  Pallas kernels  72.5 us (25%)
  local copies, waits for them, and re-layouts  32.1 us (11%)
  waiting for transfers between devices  23.8 us (8%)
    all_to_all x1, blocking collectives, send_grads(): return lax.all_to_all(pair, ('dp', *SPACE), 0, 0, tiled=True)  41 us
    all_to_all x1, blocking collectives, per_device(): whole = lax.all_to_all(copies, SPACE, 0, 0, tiled=True)  34.6 us
    unnamed x100, local copies, waits for them, and re-layouts  27.9 us
    ppermute x7, starting transfers between devices, swapped(): return lax.ppermute(value, axis, [(0, 1), (1, 0)])  16.5 us
    ppermute x4, starting transfers between devices, from_rows(): above = lax.ppermute(bottom, RANKS, FORWARD['rows'])  14.8 us
    pallas_call x2, Pallas kernels, mlp(): call(functools.partial(mlp_body, k), outs, 12, 60000000, scalars=1)  13.3 us
    ppermute x4, starting transfers between devices, from_columns(): left = lax.ppermute(to_high, 'z', FORWARD['z'])  12.4 us
    pallas_call x2, Pallas kernels, tap_grads(): return call(taps_body, [((49 * 4, 128), F32)], 2, 40000000)(seen, grads)[0]  12.1 us
  transfers between devices with their start and end apart: 28, of which 9 were waited for; matrix products, arithmetic and copies ran while one was open for 1% of the time, Pallas kernels for 17%

profile of v1, /device:TPU:1, one launch (start us, length us, event | category | flops | bytes accessed | tf_op | source)
XLA Modules:
  0.0 280.4 jit_solution(2125450105308083268)
XLA Ops:
  1.8 4.6 %collective-permute-start = (bf16[96,512]{1,0:T(8,128)(2,1)S(1)}, bf16[96,512]{1,0:T(8,128)(2,1)S(1)}, u32[]{:S(2)}, u32[]{:S(2)}) collective-permute-start(bf16[96,512]{1,0:T(8,128)(2,1)S(1)} %bitcast.29), channel_id=1, source_target_pairs={{0,8},{8,16},{16,24},{24,32},{32,40},{40,48},{48,56},{56,64},{64,7... | collective-permute-start | bytes 294920 | tf_op jit(solution)/shard_map/ppermute | solution.py:463
  6.4 1.9 collective-permute-start.1
  8.3 1.9 dynamic-slice_bitcast_fusion.2
  10.2 2.5 collective-permute-start.6
  14.0 3.5 %collective-permute-start.2 = (bf16[336,128]{1,0:T(8,128)(2,1)S(1)}, bf16[336,128]{1,0:T(8,128)(2,1)S(1)}, u32[]{:S(2)}, u32[]{:S(2)}) collective-permute-start(bf16[336,128]{1,0:T(8,128)(2,1)S(1)} %get-tuple-element.67), channel_id=1, source_target_pairs={{0,2},{2,4},{4,6},{1,3},{3,5},{5,7},{8,10},{10,12},{12,14},{9,11},... | collective-permute-start | bytes 258056 | tf_op jit(solution)/shard_map/ppermute | solution.py:469
  19.8 3.1 %collective-permute-done.3.right = bf16[336,128]{1,0:T(8,128)(2,1)S(1)} collective-permute-done((bf16[336,128]{1,0:T(8,128)(2,1)S(1)}, bf16[336,128]{1,0:T(8,128)(2,1)S(1)}, u32[]{:S(2)}, u32[]{:S(2)}) %collective-permute-start.3) | collective-permute-done | bytes 86048 | tf_op jit(solution)/shard_map/ppermute | solution.py:470
  25.0 5.1 %shard_map.163 = (f32[4480,128]{1,0:T(8,128)S(1)}, bf16[512,512]{1,0:T(8,128)(2,1)S(1)}, f32[512,512]{1,0:T(8,128)S(1)}, f32[512,128]{1,0:T(8,128)S(1)}) custom-call(f32[4480,128]{1,0:T(8,128)S(1)} %get-tuple-element.66.old, bf16[336,128]{1,0:T(8,128)(2,1)S(1)} %collective-permute-done.2.left, bf16[336,128]{1,0:T(8,128)(2,1)S(1)} %collective-permute-done.3.right, ...), custom_call_target="tpu_custom_call" | custom-call | flops 40000000 | bytes 4000000 | tf_op jit(solution)/shard_map/pallas_call | solution.py:374
  34.5 2.6 collective-permute-start.14
  37.2 5.2 %collective-permute-start.7 = (bf16[1024,256]{1,0:T(8,128)(2,1)S(1)}, bf16[1024,256]{1,0:T(8,128)(2,1)}, u32[]{:S(2)}, u32[]{:S(2)}) collective-permute-start(bf16[1024,256]{1,0:T(8,128)(2,1)S(1)} %collective-permute-done.6.got_out), channel_id=1, source_target_pairs={{0,8},{8,0},{1,9},{9,1},{2,10},{10,2},{3,11},{11,3},{4,12},{12,4},... | collective-permute-start | bytes 1572872 | tf_op jit(solution)/shard_map/ppermute | solution.py:475
  44.2 5.3 %collective-permute-start.15 = (bf16[1024,256]{1,0:T(8,128)(2,1)}, bf16[1024,256]{1,0:T(8,128)(2,1)}, u32[]{:S(2)}, u32[]{:S(2)}) collective-permute-start(bf16[1024,256]{1,0:T(8,128)(2,1)} %collective-permute-done.14.got_out), channel_id=1, source_target_pairs={{0,8},{8,0},{1,9},{9,1},{2,10},{10,2},{3,11},{11,3},{4,12},{12,4},... | collective-permute-start | bytes 1572872 | tf_op jit(solution)/shard_map/ppermute | solution.py:475
  49.5 3.3 %collective-permute-start.13 = (bf16[128,2048]{1,0:T(8,128)(2,1)}, bf16[128,2048]{1,0:T(8,128)(2,1)}, u32[]{:S(2)}, u32[]{:S(2)}) collective-permute-start(bf16[128,2048]{1,0:T(8,128)(2,1)} %collective-permute-done.12.got_in), channel_id=1, source_target_pairs={{0,8},{8,0},{1,9},{9,1},{2,10},{10,2},{3,11},{11,3},{4,12},{12,4},... | collective-permute-start | bytes 1572872 | tf_op jit(solution)/shard_map/ppermute | solution.py:475
  53.0 1.6 copy-done.1
  56.7 6.2 %shard_map.164 = (bf16[512,512]{1,0:T(8,128)(2,1)S(1)}, bf16[96,512]{1,0:T(8,128)(2,1)S(1)}, bf16[96,512]{1,0:T(8,128)(2,1)S(1)}, bf16[512,2048]{1,0:T(8,128)(2,...) custom-call(s32[2]{0:T(128)S(1)} %pad_add_fusion.place, ...), custom_call_target="tpu_custom_call" | custom-call | flops 60000000 | bytes 4000000 | tf_op jit(solution)/shard_map/pallas_call | solution.py:384
  65.5 1.4 copy-done.12
  68.2 3.9 %collective-permute-start.8 = (bf16[96,512]{1,0:T(8,128)(2,1)S(1)}, bf16[96,512]{1,0:T(8,128)(2,1)S(1)}, u32[]{:S(2)}, u32[]{:S(2)}) collective-permute-start(bf16[96,512]{1,0:T(8,128)(2,1)S(1)} %get-tuple-element.71), channel_id=1, source_target_pairs={{0,8},{8,16},{16,24},{24,32},{32,40},{40,48},{48,56},{56,64},{64,7... | collective-permute-start | bytes 294920 | tf_op jit(solution)/shard_map/ppermute | solution.py:463
  72.2 1.9 collective-permute-start.9
  74.1 4.0 %collective-permute-done.9.bottom = bf16[96,512]{1,0:T(8,128)(2,1)S(1)} collective-permute-done((bf16[96,512]{1,0:T(8,128)(2,1)S(1)}, bf16[96,512]{1,0:T(8,128)(2,1)S(1)}, u32[]{:S(2)}, u32[]{:S(2)}) %collective-permute-start.9) | collective-permute-done | bytes 98336 | tf_op jit(solution)/shard_map/ppermute | solution.py:464
  78.4 3.5 %collective-permute-start.10 = (bf16[336,128]{1,0:T(8,128)(2,1)S(1)}, bf16[336,128]{1,0:T(8,128)(2,1)S(1)}, u32[]{:S(2)}, u32[]{:S(2)}) collective-permute-start(bf16[336,128]{1,0:T(8,128)(2,1)S(1)} %get-tuple-element.74), channel_id=1, source_target_pairs={{0,2},{2,4},{4,6},{1,3},{3,5},{5,7},{8,10},{10,12},{12,14},{9,11},... | collective-permute-start | bytes 258056 | tf_op jit(solution)/shard_map/ppermute | solution.py:469
  81.9 1.5 collective-permute-start.11
  83.4 3.7 %collective-permute-done.11.right = bf16[336,128]{1,0:T(8,128)(2,1)S(1)} collective-permute-done((bf16[336,128]{1,0:T(8,128)(2,1)S(1)}, bf16[336,128]{1,0:T(8,128)(2,1)S(1)}, u32[]{:S(2)}, u32[]{:S(2)}) %collective-permute-start.11) | collective-permute-done | bytes 86048 | tf_op jit(solution)/shard_map/ppermute | solution.py:470
  87.2 5.4 %shard_map.166 = (f32[4480,128]{1,0:T(8,128)S(1)}, bf16[512,512]{1,0:T(8,128)(2,1)S(1)}, f32[512,512]{1,0:T(8,128)S(1)}, f32[512,128]{1,0:T(8,128)S(1)}) custom-call(f32[4480,128]{1,0:T(8,128)S(1)} %get-tuple-element.73.old, bf16[336,128]{1,0:T(8,128)(2,1)S(1)} %collective-permute-done.10.left, bf16[336,128]{1,0:T(8,128)(2,1)S(1)} %collective-permute-done.11.right, ...), custom_call_target="tpu_custom_call" | custom-call | flops 40000000 | bytes 4000000 | tf_op jit(solution)/shard_map/pallas_call | solution.py:374
  92.7 7.2 %shard_map.167 = (bf16[512,512]{1,0:T(8,128)(2,1)}, bf16[96,512]{1,0:T(8,128)(2,1)}, bf16[96,512]{1,0:T(8,128)(2,1)}, bf16[512,2048]{1,0:T(8,128)(2,1)S(1)}, bf1...) custom-call(s32[2]{0:T(128)S(1)} %pad_add_fusion.place, ...), custom_call_target="tpu_custom_call" | custom-call | flops 60000000 | bytes 4000000 | tf_op jit(solution)/shard_map/pallas_call | solution.py:384
  99.8 2.8 %shard_map.168 = (bf16[512,512]{1,0:T(8,128)(2,1)S(1)}, bf16[512,2048]{1,0:T(8,128)(2,1)S(1)}, f32[4480,128]{1,0:T(8,128)S(1)}, bf16[96,512]{1,0:T(8,128)(2,1)S(...) custom-call(bf16[512,512]{1,0:T(8,128)(2,1)S(1)} %bitcast.25, ...), custom_call_target="tpu_custom_call" | custom-call | flops 60000000 | bytes 4000000 | tf_op jit(solution)/shard_map/pallas_call | solution.py:395
  102.7 3.0 %shard_map.177 = (bf16[512,2048]{1,0:T(8,128)(2,1)S(1)}, bf16[512,2048]{1,0:T(8,128)(2,1)S(1)}) custom-call(s32[2]{0:T(128)S(1)} %pad_add_fusion.place, bf16[512,512]{1,0:T(8,128)(2,1)S(1)} %get-tuple-element.76.normal, bf16[512,512]{1,0:T(8,128)(2,1)S(1)} %get-tuple-element.112.low, bf16[512,2048]{1,0:T(8,128)(2,1)S(1)} %get-tuple-element.113.act, ...), custom_call_target="tpu_custom_call" | custom-call | flops 50000000 | bytes 4000000 | tf_op jit(solution)/shard_map/pallas_call | solution.py:402
  105.8 4.1 %collective-permute-start.16 = (bf16[96,512]{1,0:T(8,128)(2,1)S(1)}, bf16[96,512]{1,0:T(8,128)(2,1)S(1)}, u32[]{:S(2)}, u32[]{:S(2)}) collective-permute-start(bf16[96,512]{1,0:T(8,128)(2,1)S(1)} %get-tuple-element.87), channel_id=1, source_target_pairs={{0,8},{8,16},{16,24},{24,32},{32,40},{40,48},{48,56},{56,64},{64,7... | collective-permute-start | bytes 294920 | tf_op jit(solution)/shard_map/ppermute | solution.py:463
  110.0 1.9 collective-permute-start.17
  111.9 4.0 %collective-permute-done.17.bottom = bf16[96,512]{1,0:T(8,128)(2,1)S(1)} collective-permute-done((bf16[96,512]{1,0:T(8,128)(2,1)S(1)}, bf16[96,512]{1,0:T(8,128)(2,1)S(1)}, u32[]{:S(2)}, u32[]{:S(2)}) %collective-permute-start.17) | collective-permute-done | bytes 98336 | tf_op jit(solution)/shard_map/ppermute | solution.py:464
  116.1 3.3 %collective-permute-start.18 = (bf16[336,128]{1,0:T(8,128)(2,1)S(1)}, bf16[336,128]{1,0:T(8,128)(2,1)S(1)}, u32[]{:S(2)}, u32[]{:S(2)}) collective-permute-start(bf16[336,128]{1,0:T(8,128)(2,1)S(1)} %get-tuple-element.90), channel_id=1, source_target_pairs={{0,2},{2,4},{4,6},{1,3},{3,5},{5,7},{8,10},{10,12},{12,14},{9,11},... | collective-permute-start | bytes 258056 | tf_op jit(solution)/shard_map/ppermute | solution.py:469
  120.7 6.0 %shard_map.178.taps = f32[196,128]{1,0:T(8,128)S(1)} custom-call(f32[4480,128]{1,0:T(8,128)S(1)} %get-tuple-element.117.seen, f32[4480,128]{1,0:T(8,128)S(1)} %get-tuple-element.86.old.grads), custom_call_target="tpu_custom_call" | custom-call | flops 40000000 | bytes 4000000 | tf_op jit(solution)/shard_map/pallas_call | solution.py:406
  126.7 1.9 shard_map.179
  128.7 12.0 %all-to-all-start.1 = ((bf16[64,8,2176]{2,1,0:T(8,128)(2,1)}), bf16[64,8,2176]{2,1,0:T(8,128)(2,1)}, u32[]{:S(2)}, u32[]{:S(2)}) async-start(bf16[64,8,2176]{2,1,0:T(8,128)(2,1)} %shard_map.179), calls=%async_computation.1 | async-start | bytes 4456448 | tf_op jit(solution)/shard_map/all_to_all | solution.py:497
  144.8 4.8 %shard_map.170.u = f32[512,512]{1,0:T(8,128)S(1)} custom-call(f32[4480,128]{1,0:T(8,128)S(1)} %get-tuple-element.89.old, bf16[336,128]{1,0:T(8,128)(2,1)S(1)} %copy-done.30, bf16[336,128]{1,0:T(8,128)(2,1)S(1)} %copy-done.32, f32[7,7,2,512]{3,2,1,0:T(2,128)S(1)} %bitcast.21, bf16[512,512]{1,0:T(8,128)(2,1)S(1)} %bitcast.26), custom_call_target="tpu_custom_call" | custom-call | flops 40000000 | bytes 4000000 | tf_op jit(solution)/shard_map/pallas_call | solution.py:411
  149.6 1.6 copy-done.15
  154.6 2.9 %shard_map.171 = (bf16[512,512]{1,0:T(8,128)(2,1)S(1)}, bf16[512,2048]{1,0:T(8,128)(2,1)S(1)}, f32[4480,128]{1,0:T(8,128)S(1)}, bf16[96,512]{1,0:T(8,128)(2,1)S(...) custom-call(f32[512,512]{1,0:T(8,128)S(1)} %shard_map.170.u, ...), custom_call_target="tpu_custom_call" | custom-call | flops 60000000 | bytes 4000000 | tf_op jit(solution)/shard_map/pallas_call | solution.py:395
  158.8 3.0 %shard_map.174 = (bf16[512,2048]{1,0:T(8,128)(2,1)S(1)}, bf16[512,2048]{1,0:T(8,128)(2,1)S(1)}) custom-call(s32[2]{0:T(128)S(1)} %copy-done.44, bf16[512,512]{1,0:T(8,128)(2,1)S(1)} %copy-done.18, bf16[512,512]{1,0:T(8,128)(2,1)S(1)} %get-tuple-element.104.low, bf16[512,2048]{1,0:T(8,128)(2,1)S(1)} %copy-done.9, bf16[512,2048]{1,0:T(8,128)(2,1)S(1)} %get-tuple-element.106.gh), custom_call_target="tpu_custom_call" | custom-call | flops 50000000 | bytes 4000000 | tf_op jit(solution)/shard_map/pallas_call | solution.py:402
  161.9 6.0 %shard_map.175.taps = f32[196,128]{1,0:T(8,128)S(1)} custom-call(f32[4480,128]{1,0:T(8,128)S(1)} %copy-done.7, f32[4480,128]{1,0:T(8,128)S(1)} %get-tuple-element.98.old.grads), custom_call_target="tpu_custom_call" | custom-call | flops 40000000 | bytes 4000000 | tf_op jit(solution)/shard_map/pallas_call | solution.py:406
  170.2 41.0 %all_to_all.15.pieces0 = bf16[64,8,2176]{2,1,0:T(8,128)(2,1)S(1)} all-to-all(bf16[64,8,2176]{2,1,0:T(8,128)(2,1)} %copy-done.2), channel_id=1, replica_groups=mesh['xh'=2,'y'=4,'core'=2,'z'=4,'dp'=2] {'dp','xh','y','z'}, dimensions={0} | all-to-all | bytes 4456448 | tf_op jit(solution)/shard_map/all_to_all | solution.py:497
  211.1 2.9 %shard_map.180 = bf16[32,8,4352]{2,1,0:T(8,128)(2,1)S(1)} custom-call(bf16[64,8,2176]{2,1,0:T(8,128)(2,1)S(1)} %all_to_all.15.pieces0, bf16[64,8,2176]{2,1,0:T(8,128)(2,1)} %all-to-all-done.1.pieces1), custom_call_target="tpu_custom_call" | custom-call | flops 5000000 | bytes 4000000 | tf_op jit(solution)/shard_map/pallas_call | solution.py:548
  214.0 34.6 %all_to_all.16.whole.whole0.whole1 = bf16[32,8,4352]{2,1,0:T(8,128)(2,1)S(1)} all-to-all(bf16[32,8,4352]{2,1,0:T(8,128)(2,1)S(1)} %shard_map.180), channel_id=1, replica_groups=mesh['xh'=2,'y'=4,'core'=2,'z'=4,'dp'=2] {'xh','y','z'}, dimensions={0} | all-to-all | bytes 4456448 | tf_op jit(solution)/shard_map/all_to_all | solution.py:549
  248.6 2.6 collective-permute-start.26
  251.2 2.1 collective-permute-start.20
  253.3 2.2 collective-permute-start.21
  255.5 3.7 %collective-permute-done.21.bottom = bf16[96,512]{1,0:T(8,128)(2,1)S(1)} collective-permute-done((bf16[96,512]{1,0:T(8,128)(2,1)S(1)}, bf16[96,512]{1,0:T(8,128)(2,1)S(1)}, u32[]{:S(2)}, u32[]{:S(2)}) %collective-permute-start.21) | collective-permute-done | bytes 98336 | tf_op jit(solution)/shard_map/ppermute | solution.py:464
  259.5 2.0 collective-permute-start.22
  263.0 3.7 %collective-permute-done.23.right = bf16[336,128]{1,0:T(8,128)(2,1)S(1)} collective-permute-done((bf16[336,128]{1,0:T(8,128)(2,1)S(1)}, bf16[336,128]{1,0:T(8,128)(2,1)S(1)}, u32[]{:S(2)}, u32[]{:S(2)}) %collective-permute-start.23) | collective-permute-done | bytes 86048 | tf_op jit(solution)/shard_map/ppermute | solution.py:470
  266.8 5.6 %shard_map.173 = bf16[512,512]{1,0:T(8,128)(2,1)} custom-call(f32[4480,128]{1,0:T(8,128)S(1)} %get-tuple-element.101.old, bf16[336,128]{1,0:T(8,128)(2,1)S(1)} %collective-permute-done.22.left, bf16[336,128]{1,0:T(8,128)(2,1)S(1)} %collective-permute-done.23.right, f32[7,7,2,512]{3,2,1,0:T(2,128)S(1)} %bitcast.22, f32[512,512]{1,0:T(8,128)S(1)} %shard_map.170.u), custom_call_target="tpu_custom_call" | custom-call | flops 40000000 | bytes 4000000 | tf_op jit(solution)/shard_map/pallas_call | solution.py:411
  272.4 1.8 shard_map.182
  274.2 6.2 %shard_map.181 = (f32[2,256,2048]{2,1,0:T(8,128)}, f32[2,2048,256]{2,1,0:T(8,128)}) custom-call(s32[2]{0:T(128)} %copy-done.43, bf16[32,8,4352]{2,1,0:T(8,128)(2,1)} %copy-done.49, bf16[32,8,4352]{2,1,0:T(8,128)(2,1)} %collective-permute-done.26.mate.mate0.mate1), custom_call_target="tpu_custom_call" | custom-call | flops 10000000 | bytes 12000000 | tf_op jit(solution)/shard_map/pallas_call | solution.py:418
  (137 shorter events, 33.9 us)
Async XLA Ops:
  0.6 18.2 %copy-start = (bf16[2,256,2048]{2,1,0:T(8,128)(2,1)S(1)}, bf16[2,256,2048]{2,1,0:T(8,128)(2,1)}, u32[]{:S(2)}) copy-start(bf16[2,256,2048]{2,1,0:T(8,128)(2,1)} %own_in.3) | copy-start | bytes 6291460
  0.6 22.3 %copy-start.3 = (f32[2,7,7,512]{3,0,2,1:T(2,128)S(1)}, f32[2,7,7,512]{3,0,2,1:T(2,128)}, u32[]{:S(2)}) copy-start(f32[2,7,7,512]{3,0,2,1:T(2,128)} %param.13) | copy-start | bytes 602116
  1.8 10.9 %collective-permute-start = (bf16[96,512]{1,0:T(8,128)(2,1)S(1)}, bf16[96,512]{1,0:T(8,128)(2,1)S(1)}, u32[]{:S(2)}, u32[]{:S(2)}) collective-permute-start(bf16[96,512]{1,0:T(8,128)(2,1)S(1)} %bitcast.29), channel_id=1, source_target_pairs={{0,8},{8,16},{16,24},{24,32},{32,40},{40,48},{48,56},{56,64},{64,7... | collective-permute-start | bytes 294920 | tf_op jit(solution)/shard_map/ppermute | solution.py:463
  6.4 6.3 %collective-permute-start.1 = (bf16[96,512]{1,0:T(8,128)(2,1)S(1)}, bf16[96,512]{1,0:T(8,128)(2,1)S(1)}, u32[]{:S(2)}, u32[]{:S(2)}) collective-permute-start(bf16[96,512]{1,0:T(8,128)(2,1)S(1)} %bitcast.28), channel_id=1, source_target_pairs={{8,0},{16,8},{24,16},{32,24},{40,32},{48,40},{56,48},{64,56},{72,6... | collective-permute-start | bytes 294920 | tf_op jit(solution)/shard_map/ppermute | solution.py:464
  10.2 27.1 %collective-permute-start.6 = (bf16[1024,256]{1,0:T(8,128)(2,1)}, bf16[1024,256]{1,0:T(8,128)(2,1)S(1)}, u32[]{:S(2)}, u32[]{:S(2)}) collective-permute-start(bf16[1024,256]{1,0:T(8,128)(2,1)} %dynamic-slice_bitcast_fusion.2), channel_id=1, source_target_pairs={{0,65},{1,0},{64,1},{65,64},{2,67},{3,2},{66,3},{67,66},{4,69},{5,... | collective-permute-start | bytes 1572872 | tf_op jit(solution)/shard_map/ppermute | solution.py:479
  14.0 5.8 %collective-permute-start.2 = (bf16[336,128]{1,0:T(8,128)(2,1)S(1)}, bf16[336,128]{1,0:T(8,128)(2,1)S(1)}, u32[]{:S(2)}, u32[]{:S(2)}) collective-permute-start(bf16[336,128]{1,0:T(8,128)(2,1)S(1)} %get-tuple-element.67), channel_id=1, source_target_pairs={{0,2},{2,4},{4,6},{1,3},{3,5},{5,7},{8,10},{10,12},{12,14},{9,11},... | collective-permute-start | bytes 258056 | tf_op jit(solution)/shard_map/ppermute | solution.py:469
  17.5 5.4 %collective-permute-start.3 = (bf16[336,128]{1,0:T(8,128)(2,1)S(1)}, bf16[336,128]{1,0:T(8,128)(2,1)S(1)}, u32[]{:S(2)}, u32[]{:S(2)}) collective-permute-start(bf16[336,128]{1,0:T(8,128)(2,1)S(1)} %get-tuple-element.68), channel_id=1, source_target_pairs={{2,0},{4,2},{6,4},{3,1},{5,3},{7,5},{10,8},{12,10},{14,12},{11,9},... | collective-permute-start | bytes 258056 | tf_op jit(solution)/shard_map/ppermute | solution.py:470
  18.9 24.3 %collective-permute-start.4 = (bf16[128,2048]{1,0:T(8,128)(2,1)S(1)}, bf16[128,2048]{1,0:T(8,128)(2,1)}, u32[]{:S(2)}, u32[]{:S(2)}) collective-permute-start(bf16[128,2048]{1,0:T(8,128)(2,1)S(1)} %dynamic-slice_bitcast_fusion.3), channel_id=1, source_target_pairs={{0,1},{1,64},{64,65},{65,0},{2,3},{3,66},{66,67},{67,2},{4,5},{5,6... | collective-permute-start | bytes 1572872 | tf_op jit(solution)/shard_map/ppermute | solution.py:479
  25.0 28.0 %copy-start.5 = (bf16[1,16,32,512]{3,2,1,0:T(8,128)(2,1)S(1)}, bf16[1,16,32,512]{3,2,1,0:T(8,128)(2,1)}, u32[]{:S(2)}) copy-start(bf16[1,16,32,512]{3,2,1,0:T(8,128)(2,1)} %param.11) | copy-start | bytes 1572868
  25.0 28.0 %copy-start.33 = (f32[2,2048]{1,0:T(2,128)S(1)}, f32[2,2048]{1,0:T(2,128)}, u32[]{:S(2)}) copy-start(f32[2,2048]{1,0:T(2,128)} %bias_in.3) | copy-start | bytes 49156
  25.0 28.0 %copy-start.37 = (f32[2,512]{1,0:T(2,128)S(1)}, f32[2,512]{1,0:T(2,128)}, u32[]{:S(2)}) copy-start(f32[2,512]{1,0:T(2,128)} %scale.7) | copy-start | bytes 12292
  25.0 28.0 %copy-start.42 = (f32[2,512]{1,0:T(2,128)S(1)}, f32[2,512]{1,0:T(2,128)}, u32[]{:S(2)}) copy-start(f32[2,512]{1,0:T(2,128)} %bias_out.3) | copy-start | bytes 12292
  33.3 9.1 %copy-start.27 = (f32[512,128]{1,0:T(8,128)}, f32[512,128]{1,0:T(8,128)S(1)}, u32[]{:S(2)}) copy-start(f32[512,128]{1,0:T(8,128)S(1)} %get-tuple-element.95.rstd) | copy-start | bytes 786436
  34.5 9.7 %collective-permute-start.14 = (bf16[1024,256]{1,0:T(8,128)(2,1)S(1)}, bf16[1024,256]{1,0:T(8,128)(2,1)}, u32[]{:S(2)}, u32[]{:S(2)}) collective-permute-start(bf16[1024,256]{1,0:T(8,128)(2,1)S(1)} %dynamic-slice_bitcast_fusion), channel_id=1, source_target_pairs={{0,65},{1,0},{64,1},{65,64},{2,67},{3,2},{66,3},{67,66},{4,69},{5,... | collective-permute-start | bytes 1572872 | tf_op jit(solution)/shard_map/ppermute | solution.py:479
  37.1 12.4 %collective-permute-start.12 = (bf16[128,2048]{1,0:T(8,128)(2,1)S(1)}, bf16[128,2048]{1,0:T(8,128)(2,1)}, u32[]{:S(2)}, u32[]{:S(2)}) collective-permute-start(bf16[128,2048]{1,0:T(8,128)(2,1)S(1)} %dynamic-slice_bitcast_fusion.1), channel_id=1, source_target_pairs={{0,1},{1,64},{64,65},{65,0},{2,3},{3,66},{66,67},{67,2},{4,5},{5,6... | collective-permute-start | bytes 1572872 | tf_op jit(solution)/shard_map/ppermute | solution.py:479
  37.2 15.7 %collective-permute-start.7 = (bf16[1024,256]{1,0:T(8,128)(2,1)S(1)}, bf16[1024,256]{1,0:T(8,128)(2,1)}, u32[]{:S(2)}, u32[]{:S(2)}) collective-permute-start(bf16[1024,256]{1,0:T(8,128)(2,1)S(1)} %collective-permute-done.6.got_out), channel_id=1, source_target_pairs={{0,8},{8,0},{1,9},{9,1},{2,10},{10,2},{3,11},{11,3},{4,12},{12,4},... | collective-permute-start | bytes 1572872 | tf_op jit(solution)/shard_map/ppermute | solution.py:475
  43.2 9.8 %collective-permute-start.5 = (bf16[128,2048]{1,0:T(8,128)(2,1)}, bf16[128,2048]{1,0:T(8,128)(2,1)}, u32[]{:S(2)}, u32[]{:S(2)}) collective-permute-start(bf16[128,2048]{1,0:T(8,128)(2,1)} %collective-permute-done.4.got_in), channel_id=1, source_target_pairs={{0,8},{8,0},{1,9},{9,1},{2,10},{10,2},{3,11},{11,3},{4,12},{12,4},... | collective-permute-start | bytes 1572872 | tf_op jit(solution)/shard_map/ppermute | solution.py:475
  44.2 48.4 %collective-permute-start.15 = (bf16[1024,256]{1,0:T(8,128)(2,1)}, bf16[1024,256]{1,0:T(8,128)(2,1)}, u32[]{:S(2)}, u32[]{:S(2)}) collective-permute-start(bf16[1024,256]{1,0:T(8,128)(2,1)} %collective-permute-done.14.got_out), channel_id=1, source_target_pairs={{0,8},{8,0},{1,9},{9,1},{2,10},{10,2},{3,11},{11,3},{4,12},{12,4},... | collective-permute-start | bytes 1572872 | tf_op jit(solution)/shard_map/ppermute | solution.py:475
  49.5 43.1 %collective-permute-start.13 = (bf16[128,2048]{1,0:T(8,128)(2,1)}, bf16[128,2048]{1,0:T(8,128)(2,1)}, u32[]{:S(2)}, u32[]{:S(2)}) collective-permute-start(bf16[128,2048]{1,0:T(8,128)(2,1)} %collective-permute-done.12.got_in), channel_id=1, source_target_pairs={{0,8},{8,0},{1,9},{9,1},{2,10},{10,2},{3,11},{11,3},{4,12},{12,4},... | collective-permute-start | bytes 1572872 | tf_op jit(solution)/shard_map/ppermute | solution.py:475
  52.9 49.7 %copy-start.43 = (s32[2]{0:T(128)}, s32[2]{0:T(128)S(1)}, u32[]{:S(2)}) copy-start(s32[2]{0:T(128)S(1)} %pad_add_fusion.place) | copy-start | bytes 28
  56.7 30.5 %copy-start.36 = (f32[2,512]{1,0:T(2,128)S(1)}, f32[2,512]{1,0:T(2,128)}, u32[]{:S(2)}) copy-start(f32[2,512]{1,0:T(2,128)} %gain.7) | copy-start | bytes 12292
  56.7 30.5 %copy-start.39 = (f32[2,512]{1,0:T(2,128)S(1)}, f32[2,512]{1,0:T(2,128)}, u32[]{:S(2)}) copy-start(f32[2,512]{1,0:T(2,128)} %bias.3) | copy-start | bytes 12292
  56.7 30.5 %copy-start.41 = (f32[2,512]{1,0:T(2,128)S(1)}, f32[2,512]{1,0:T(2,128)}, u32[]{:S(2)}) copy-start(f32[2,512]{1,0:T(2,128)} %shift.3) | copy-start | bytes 12292
  68.2 24.4 %copy-start.23 = (f32[512,512]{1,0:T(8,128)}, f32[512,512]{1,0:T(8,128)S(1)}, u32[]{:S(2)}) copy-start(f32[512,512]{1,0:T(8,128)S(1)} %get-tuple-element.92.branch) | copy-start | bytes 3145732
  68.2 24.4 %copy-start.34 = (f32[2,2048]{1,0:T(2,128)S(1)}, f32[2,2048]{1,0:T(2,128)}, u32[]{:S(2)}) copy-start(f32[2,2048]{1,0:T(2,128)} %bias_in.3) | copy-start | bytes 49156
  68.2 5.9 %collective-permute-start.8 = (bf16[96,512]{1,0:T(8,128)(2,1)S(1)}, bf16[96,512]{1,0:T(8,128)(2,1)S(1)}, u32[]{:S(2)}, u32[]{:S(2)}) collective-permute-start(bf16[96,512]{1,0:T(8,128)(2,1)S(1)} %get-tuple-element.71), channel_id=1, source_target_pairs={{0,8},{8,16},{16,24},{24,32},{32,40},{40,48},{48,56},{56,64},{64,7... | collective-permute-start | bytes 294920 | tf_op jit(solution)/shard_map/ppermute | solution.py:463
  72.2 5.9 %collective-permute-start.9 = (bf16[96,512]{1,0:T(8,128)(2,1)S(1)}, bf16[96,512]{1,0:T(8,128)(2,1)S(1)}, u32[]{:S(2)}, u32[]{:S(2)}) collective-permute-start(bf16[96,512]{1,0:T(8,128)(2,1)S(1)} %get-tuple-element.72), channel_id=1, source_target_pairs={{8,0},{16,8},{24,16},{32,24},{40,32},{48,40},{56,48},{64,56},{72,6... | collective-permute-start | bytes 294920 | tf_op jit(solution)/shard_map/ppermute | solution.py:464
  78.4 5.1 %collective-permute-start.10 = (bf16[336,128]{1,0:T(8,128)(2,1)S(1)}, bf16[336,128]{1,0:T(8,128)(2,1)S(1)}, u32[]{:S(2)}, u32[]{:S(2)}) collective-permute-start(bf16[336,128]{1,0:T(8,128)(2,1)S(1)} %get-tuple-element.74), channel_id=1, source_target_pairs={{0,2},{2,4},{4,6},{1,3},{3,5},{5,7},{8,10},{10,12},{12,14},{9,11},... | collective-permute-start | bytes 258056 | tf_op jit(solution)/shard_map/ppermute | solution.py:469
  81.9 5.2 %collective-permute-start.11 = (bf16[336,128]{1,0:T(8,128)(2,1)S(1)}, bf16[336,128]{1,0:T(8,128)(2,1)S(1)}, u32[]{:S(2)}, u32[]{:S(2)}) collective-permute-start(bf16[336,128]{1,0:T(8,128)(2,1)S(1)} %get-tuple-element.75), channel_id=1, source_target_pairs={{2,0},{4,2},{6,4},{3,1},{5,3},{7,5},{10,8},{12,10},{14,12},{11,9},... | collective-permute-start | bytes 258056 | tf_op jit(solution)/shard_map/ppermute | solution.py:470
  92.6 7.2 %copy-start.19 = (bf16[1,16,32,512]{3,2,1,0:T(8,128)(2,1)S(1)}, bf16[1,16,32,512]{3,2,1,0:T(8,128)(2,1)}, u32[]{:S(2)}) copy-start(bf16[1,16,32,512]{3,2,1,0:T(8,128)(2,1)} %param.12) | copy-start | bytes 1572868
  105.7 21.0 %collective-permute-start.25 = (bf16[512,2048]{1,0:T(8,128)(2,1)S(1)}, bf16[512,2048]{1,0:T(8,128)(2,1)S(1)}, u32[]{:S(2)}, u32[]{:S(2)}) collective-permute-start(bf16[512,2048]{1,0:T(8,128)(2,1)S(1)} %get-tuple-element.116), channel_id=1, source_target_pairs={{0,8},{8,0},{1,9},{9,1},{2,10},{10,2},{3,11},{11,3},{4,12},{12,4},... | collective-permute-start | bytes 6291464 | tf_op jit(solution)/shard_map/ppermute | solution.py:475
  105.8 6.1 %collective-permute-start.16 = (bf16[96,512]{1,0:T(8,128)(2,1)S(1)}, bf16[96,512]{1,0:T(8,128)(2,1)S(1)}, u32[]{:S(2)}, u32[]{:S(2)}) collective-permute-start(bf16[96,512]{1,0:T(8,128)(2,1)S(1)} %get-tuple-element.87), channel_id=1, source_target_pairs={{0,8},{8,16},{16,24},{24,32},{32,40},{40,48},{48,56},{56,64},{64,7... | collective-permute-start | bytes 294920 | tf_op jit(solution)/shard_map/ppermute | solution.py:463
  110.0 5.9 %collective-permute-start.17 = (bf16[96,512]{1,0:T(8,128)(2,1)S(1)}, bf16[96,512]{1,0:T(8,128)(2,1)S(1)}, u32[]{:S(2)}, u32[]{:S(2)}) collective-permute-start(bf16[96,512]{1,0:T(8,128)(2,1)S(1)} %get-tuple-element.88), channel_id=1, source_target_pairs={{8,0},{16,8},{24,16},{32,24},{40,32},{48,40},{56,48},{64,56},{72,6... | collective-permute-start | bytes 294920 | tf_op jit(solution)/shard_map/ppermute | solution.py:464
  116.1 24.5 %collective-permute-start.18 = (bf16[336,128]{1,0:T(8,128)(2,1)S(1)}, bf16[336,128]{1,0:T(8,128)(2,1)S(1)}, u32[]{:S(2)}, u32[]{:S(2)}) collective-permute-start(bf16[336,128]{1,0:T(8,128)(2,1)S(1)} %get-tuple-element.90), channel_id=1, source_target_pairs={{0,2},{2,4},{4,6},{1,3},{3,5},{5,7},{8,10},{10,12},{12,14},{9,11},... | collective-permute-start | bytes 258056 | tf_op jit(solution)/shard_map/ppermute | solution.py:469
  119.4 21.9 %collective-permute-start.19 = (bf16[336,128]{1,0:T(8,128)(2,1)S(1)}, bf16[336,128]{1,0:T(8,128)(2,1)S(1)}, u32[]{:S(2)}, u32[]{:S(2)}) collective-permute-start(bf16[336,128]{1,0:T(8,128)(2,1)S(1)} %get-tuple-element.91), channel_id=1, source_target_pairs={{2,0},{4,2},{6,4},{3,1},{5,3},{7,5},{10,8},{12,10},{14,12},{11,9},... | collective-permute-start | bytes 258056 | tf_op jit(solution)/shard_map/ppermute | solution.py:470
  128.7 41.5 %all-to-all-start.1 = ((bf16[64,8,2176]{2,1,0:T(8,128)(2,1)}), bf16[64,8,2176]{2,1,0:T(8,128)(2,1)}, u32[]{:S(2)}, u32[]{:S(2)}) async-start(bf16[64,8,2176]{2,1,0:T(8,128)(2,1)} %shard_map.179), calls=%async_computation.1 | async-start | bytes 4456448 | tf_op jit(solution)/shard_map/all_to_all | solution.py:497
  144.8 4.8 %copy-start.11 = (bf16[512,2048]{1,0:T(8,128)(2,1)S(1)}, bf16[512,2048]{1,0:T(8,128)(2,1)}, u32[]{:S(2)}) copy-start(bf16[512,2048]{1,0:T(8,128)(2,1)} %copy-done.10) | copy-start | bytes 6291460
  144.8 4.8 %copy-start.13 = (bf16[512,2048]{1,0:T(8,128)(2,1)S(1)}, bf16[512,2048]{1,0:T(8,128)(2,1)}, u32[]{:S(2)}) copy-start(bf16[512,2048]{1,0:T(8,128)(2,1)} %copy-done.12) | copy-start | bytes 6291460
  154.6 4.2 %copy-start.44 = (s32[2]{0:T(128)S(1)}, s32[2]{0:T(128)}, u32[]{:S(2)}) copy-start(s32[2]{0:T(128)} %copy-done.43) | copy-start | bytes 28
  161.8 6.2 %collective-permute-start.24 = (bf16[512,2048]{1,0:T(8,128)(2,1)S(1)}, bf16[512,2048]{1,0:T(8,128)(2,1)S(1)}, u32[]{:S(2)}, u32[]{:S(2)}) collective-permute-start(bf16[512,2048]{1,0:T(8,128)(2,1)S(1)} %get-tuple-element.108), channel_id=1, source_target_pairs={{0,8},{8,0},{1,9},{9,1},{2,10},{10,2},{3,11},{11,3},{4,12},{12,4},... | collective-permute-start | bytes 6291464 | tf_op jit(solution)/shard_map/ppermute | solution.py:475
  214.0 37.2 %copy-start.48 = (bf16[96,512]{1,0:T(8,128)(2,1)S(1)}, bf16[96,512]{1,0:T(8,128)(2,1)}, u32[]{:S(2)}) copy-start(bf16[96,512]{1,0:T(8,128)(2,1)} %copy-done.47) | copy-start | bytes 294916
  214.0 39.3 %copy-start.46 = (bf16[96,512]{1,0:T(8,128)(2,1)S(1)}, bf16[96,512]{1,0:T(8,128)(2,1)}, u32[]{:S(2)}) copy-start(bf16[96,512]{1,0:T(8,128)(2,1)} %copy-done.45) | copy-start | bytes 294916
  248.6 23.8 %copy-start.49 = (bf16[32,8,4352]{2,1,0:T(8,128)(2,1)}, bf16[32,8,4352]{2,1,0:T(8,128)(2,1)S(1)}, u32[]{:S(2)}) copy-start(bf16[32,8,4352]{2,1,0:T(8,128)(2,1)S(1)} %all_to_all.16.whole.whole0.whole1) | copy-start | bytes 6684676
  248.6 23.8 %collective-permute-start.26 = (bf16[32,8,4352]{2,1,0:T(8,128)(2,1)S(1)}, bf16[32,8,4352]{2,1,0:T(8,128)(2,1)}, u32[]{:S(2)}, u32[]{:S(2)}) collective-permute-start(bf16[32,8,4352]{2,1,0:T(8,128)(2,1)S(1)} %all_to_all.16.whole.whole0.whole1), channel_id=1, source_target_pairs={{0,8},{8,0},{1,9},{9,1},{2,10},{10,2},{3,11},{11,3},{4,12},{12,4},... | collective-permute-start | bytes 6684680 | tf_op jit(solution)/shard_map/ppermute | solution.py:475
  251.2 4.3 %collective-permute-start.20 = (bf16[96,512]{1,0:T(8,128)(2,1)S(1)}, bf16[96,512]{1,0:T(8,128)(2,1)S(1)}, u32[]{:S(2)}, u32[]{:S(2)}) collective-permute-start(bf16[96,512]{1,0:T(8,128)(2,1)S(1)} %copy-done.48), channel_id=1, source_target_pairs={{0,8},{8,16},{16,24},{24,32},{32,40},{40,48},{48,56},{56,64},{64,7... | collective-permute-start | bytes 294920 | tf_op jit(solution)/shard_map/ppermute | solution.py:463
  253.3 5.9 %collective-permute-start.21 = (bf16[96,512]{1,0:T(8,128)(2,1)S(1)}, bf16[96,512]{1,0:T(8,128)(2,1)S(1)}, u32[]{:S(2)}, u32[]{:S(2)}) collective-permute-start(bf16[96,512]{1,0:T(8,128)(2,1)S(1)} %copy-done.46), channel_id=1, source_target_pairs={{8,0},{16,8},{24,16},{32,24},{40,32},{48,40},{56,48},{64,56},{72,6... | collective-permute-start | bytes 294920 | tf_op jit(solution)/shard_map/ppermute | solution.py:464
  259.5 3.6 %collective-permute-start.22 = (bf16[336,128]{1,0:T(8,128)(2,1)S(1)}, bf16[336,128]{1,0:T(8,128)(2,1)S(1)}, u32[]{:S(2)}, u32[]{:S(2)}) collective-permute-start(bf16[336,128]{1,0:T(8,128)(2,1)S(1)} %get-tuple-element.102), channel_id=1, source_target_pairs={{0,2},{2,4},{4,6},{1,3},{3,5},{5,7},{8,10},{10,12},{12,14},{9,11},... | collective-permute-start | bytes 258056 | tf_op jit(solution)/shard_map/ppermute | solution.py:469
  261.5 5.2 %collective-permute-start.23 = (bf16[336,128]{1,0:T(8,128)(2,1)S(1)}, bf16[336,128]{1,0:T(8,128)(2,1)S(1)}, u32[]{:S(2)}, u32[]{:S(2)}) collective-permute-start(bf16[336,128]{1,0:T(8,128)(2,1)S(1)} %get-tuple-element.103), channel_id=1, source_target_pairs={{2,0},{4,2},{6,4},{3,1},{5,3},{7,5},{10,8},{12,10},{14,12},{11,9},... | collective-permute-start | bytes 258056 | tf_op jit(solution)/shard_map/ppermute | solution.py:470
  (30 other events, 39.3 us)
